TPU v7x, 32 devices: a whole 2x2x4 slice. The times are simulated.
32 devices in a mesh: tm: 4 (over y, core), lat: 8 (over z, x).
Axes of the slice: x: 2, y: 2, z: 4, core: 2. Of those that a mesh axis runs over, the one named last changes fastest.
Arguments:
- trajectory: float32 [4, 32, 64, 2048], P('tm', 'lat'), may hold values from -6 to 6
- diffusivity: float32 [4, 32, 64, 2048], P('tm', 'lat'), may hold values from 0.02 to 0.24
- adjoint_end: bfloat16 [32, 64, 2048], P('lat'), may hold values from -6 to 6
- obs_jac: bfloat16 [3072, 128, 128], P(('tm', 'lat')), may hold values from -0.5 to 0.5
- obs_value: float32 [3072, 128], P(('tm', 'lat')), may hold values from -6 to 6
- obs_weight: float32 [3072, 128], P(('tm', 'lat')), may hold values from 0.3 to 3
- obs_valid: int32 [3072, 128], P(('tm', 'lat')), may hold values 0 or 1
- obs_owner: int32 [3072, 1], P(('tm', 'lat')), may hold values from 0 to 31; in each aligned block of 96 rows (0 to 95, 96 to 191, ...) at most 6 rows name the same one
- obs_tile: int32 [3072], P(('tm', 'lat')), may hold values from 0 to 4095
Outputs:
- adjoint: float32 [4, 32, 64, 2048], P('tm', 'lat')
Inputs may be any that keep to these rules, and one draw needn't show every extreme that they name: `obs_owner`: among the 96 blocks of one device, no owner is named more than 6 times, a bound that some block reaches.
All inputs are finite; a program needn't handle non-finite values. No bound on the sum of `obs_valid` on one device may be relied on, other than what follows from the above.
Results may differ from a plain program's by a relative error of at most 0.0024.
Values may be sent and summed in bfloat16 or wider, within the bound.
A program may use at most 128 MiB of HBM per device.

v0:
```python
import jax
import jax.numpy as jnp
from jax import lax
from jax.sharding import PartitionSpec as P

TW = 2
SUB = 2


def extended(block, sides, width):
    for axis, dim in sides:
        count = lax.axis_size(axis)
        forward = [(i, i + 1) for i in range(count - 1)]
        backward = [(target, source) for source, target in forward]
        low = lax.ppermute(
            lax.slice_in_dim(block, block.shape[dim] - width, None, axis=dim), axis, forward
        )
        high = lax.ppermute(lax.slice_in_dim(block, 0, width, axis=dim), axis, backward)
        block = jnp.concatenate([low, block, high], axis=dim)
    return block


def passed_along(block, axis, distance):
    devices = range(lax.axis_size(axis))
    route = [(i - distance, i) for i in devices if i - distance in devices]
    return lax.ppermute(block, axis, route)


def block_terms(jac, state, value, weight):
    jac_f = jac.astype(jnp.float32)
    pred = jnp.einsum("bct,bt->bc", jac_f, state, precision=lax.Precision.HIGHEST)
    resid = weight * (value - pred)
    return jnp.einsum("bct,bc->bt", jac_f, resid, precision=lax.Precision.HIGHEST)


def wrap_pad(values, width, axis_pos):
    last = values.shape[axis_pos]
    left = lax.slice_in_dim(values, last - width, last, axis=axis_pos)
    right = lax.slice_in_dim(values, 0, width, axis=axis_pos)
    return jnp.concatenate([left, values, right], axis=axis_pos)


def lon_edges_one(weighted):
    return wrap_pad(weighted, 1, 2)


def propagate(field, coeffs):
    for step in range(SUB):
        weighted = coeffs * field
        padded = extended(weighted, (("lat", 0),), 1)
        sides = lon_edges_one(weighted)
        field = (
            field + padded[2:] + padded[:-2] + sides[:, :, 2:] + sides[:, :, :-2] - 4.0 * weighted
        )
    return field


def per_device(
    trajectory,
    diffusivity,
    adjoint_end,
    obs_jac,
    obs_value,
    obs_weight,
    obs_valid,
    obs_owner,
    obs_tile,
):
    traj = trajectory[0]
    lat_dev, levels, nlon = traj.shape
    per_row = nlon // TW
    tile_len = levels * TW
    devices = lax.axis_size("tm") * lax.axis_size("lat")
    blocks = obs_owner.shape[0]
    slots = max(2, 2 * blocks // devices)
    count = devices * slots
    states = (
        traj.reshape(lat_dev, levels, per_row, TW)
        .transpose(0, 2, 1, 3)
        .reshape(lat_dev * per_row, tile_len)
    )
    target = obs_owner[:, 0]
    onehot = (target[:, None] == jnp.arange(devices, dtype=jnp.int32)[None, :]).astype(jnp.int32)
    rank = jnp.sum(onehot * (jnp.cumsum(onehot, 0) - 1), 1)
    slot = target * slots + rank

    def place(values):
        buffer = jnp.zeros((count,) + values.shape[1:], values.dtype).at[slot].set(values)
        return buffer.reshape((devices, slots) + values.shape[1:])

    weights = obs_weight * obs_valid.astype(jnp.float32)
    tile_ids = lax.all_to_all(
        place(obs_tile), ("tm", "lat"), split_axis=0, concat_axis=0, tiled=True
    ).reshape(count)
    found = states[tile_ids].reshape(devices, slots, tile_len)
    returned = lax.all_to_all(
        found, ("tm", "lat"), split_axis=0, concat_axis=0, tiled=True
    ).reshape(count, tile_len)
    mine = returned[slot]
    terms = block_terms(obs_jac, mine, obs_value, weights)
    received = lax.all_to_all(
        place(terms), ("tm", "lat"), split_axis=0, concat_axis=0, tiled=True
    ).reshape(count, tile_len)
    forcing = jnp.zeros((lat_dev * per_row, tile_len), jnp.float32).at[tile_ids].add(received)
    forcing = (
        forcing.reshape(lat_dev, per_row, levels, TW)
        .transpose(0, 2, 1, 3)
        .reshape(lat_dev, levels, nlon)
    )
    section_count = lax.axis_size("tm")
    coeff_own = diffusivity[0]
    is_last = lax.axis_index("tm") == section_count - 1

    def advance(step, current):
        handed = passed_along(current.astype(jnp.bfloat16), "tm", -1)
        incoming = jnp.where(is_last, adjoint_end, handed).astype(jnp.float32)
        return forcing + propagate(incoming, coeff_own)

    result = lax.fori_loop(0, section_count, advance, forcing)
    return result[None]


def solution(mesh):
    in_specs = (
        P("tm", "lat", None, None),
        P("tm", "lat", None, None),
        P("lat", None, None),
        P(("tm", "lat"), None, None),
        P(("tm", "lat"), None),
        P(("tm", "lat"), None),
        P(("tm", "lat"), None),
        P(("tm", "lat"), None),
        P(("tm", "lat")),
    )
    out_specs = P("tm", "lat", None, None)
    return jax.shard_map(
        per_device, mesh=mesh, in_specs=in_specs, out_specs=out_specs, check_vma=False
    )
```

profile of v0, /device:TPU:28, one launch (start us, length us, event | category | flops | bytes accessed | tf_op | source)
XLA Modules:
  0.0 388.2 jit_solution(13552812722194581030)
XLA Ops:
  4.3 5.8 %all-to-all-start = ((s32[32,1,6]{2,1,0:T(1,128)}), s32[32,1,6]{2,1,0:T(1,128)S(1)}, u32[]{:S(2)}, u32[]{:S(2)}) async-start(s32[32,1,6]{2,1,0:T(1,128)} %bitcast.3), calls=%async_computation | async-start | bytes 32768 | tf_op jit(solution)/shard_map/all_to_all | solution.py:92
  10.1 3.8 copy.25
  13.9 6.7 %copy.26 = f32[4,1024,64,2]{1,0,3,2:T(4,128)} copy(f32[4,1024,64,2]{2,3,1,0:T(2,128)} %bitcast.41) | data formatting | bytes 4194304 | tf_op jit(solution)/shard_map/transpose | solution.py:79
  20.6 4.6 %copy.36 = f32[16,8,4,1024]{3,1,2,0:T(8,128)} copy(f32[16,8,4,1024]{3,2,1,0:T(4,128)} %bitcast.42) | data formatting | bytes 4194304
  32.4 5.8 %all-to-all-start.1 = ((f32[32,6,128]{2,1,0:T(8,128)}), f32[32,6,128]{2,1,0:T(8,128)S(1)}, u32[]{:S(2)}, u32[]{:S(2)}) async-start(f32[32,6,128]{2,1,0:T(8,128)} %reshape.60), calls=%async_computation.1 | async-start | bytes 262144 | tf_op jit(solution)/shard_map/all_to_all | solution.py:96
  38.2 5.2 %all-to-all-done.1 = f32[32,6,128]{2,1,0:T(8,128)S(1)} async-done(((f32[32,6,128]{2,1,0:T(8,128)}), f32[32,6,128]{2,1,0:T(8,128)S(1)}, u32[]{:S(2)}, u32[]{:S(2)}) %all-to-all-start.1) | async-done | bytes 98336 | tf_op jit(solution)/shard_map/all_to_all | solution.py:96
  44.1 5.0 %fusion.23 = f32[96,1,128]{2,1,0:T(1,128)S(1)} fusion(f32[96,128,1]{1,2,0:T(1,128)S(1)} %bitcast.45, bf16[96,128,128]{2,1,0:T(8,128)(2,1)S(1)} %copy-done), kind=kOutput, calls=%fused_computation.47 | convolution fusion | flops 18874368 | bytes 3244032 | tf_op jit(solution)/shard_map/bct,bt->bc/dot_general | solution.py:31
  53.1 5.1 %all-to-all-start.2 = ((f32[32,6,128]{2,1,0:T(8,128)}), f32[32,6,128]{2,1,0:T(8,128)S(1)}, u32[]{:S(2)}, u32[]{:S(2)}) async-start(f32[32,6,128]{2,1,0:T(8,128)} %reshape.62), calls=%async_computation.2 | async-start | bytes 262144 | tf_op jit(solution)/shard_map/all_to_all | solution.py:101
  58.3 5.1 %all-to-all-done.2 = f32[32,6,128]{2,1,0:T(8,128)S(1)} async-done(((f32[32,6,128]{2,1,0:T(8,128)}), f32[32,6,128]{2,1,0:T(8,128)S(1)}, u32[]{:S(2)}, u32[]{:S(2)}) %all-to-all-start.2) | async-done | bytes 98336 | tf_op jit(solution)/shard_map/all_to_all | solution.py:101
  69.1 3.6 reshape.64
  72.8 6.7 %copy.29 = f32[4,64,1024,2]{1,3,2,0:T(2,128)} copy(f32[4,64,1024,2]{2,0,3,1:T(4,128)} %bitcast.43) | data formatting | bytes 4194304 | tf_op jit(solution)/shard_map/transpose | solution.py:107
  79.4 3.8 copy.30
  86.4 301.7 %while.10 = (s32[]{:T(128)}, f32[4,64,2048]{2,1,0:T(8,128)}, pred[]{:T(512)}, bf16[4,64,2048]{2,1,0:T(8,128)(2,1)}, f32[4,64,2048]{2,1,0:T(8,128)}, /*index=5*/f32[4,64,2048]{2,1,0:T(8,128)}, s32[]{:T(128)}) while((s32[]{:T(128)}, f32[4,64,2048]{2,1,0:T(8,128)}, pred[]{:T(512)}, bf16[4,64,2048]{2,1,0:T(8,128)(2,1)}, f32[4,64,2048]{2,1,0:T(8,128)}, ...), condition=%wide.region_6.7_spmd, body=%wide.region_5.6_spmd.sunk | while | flops 20971520 | bytes 85998040 | solution.py:119
  90.3 12.3 %collective-permute-done = bf16[4,64,2048]{2,1,0:T(8,128)(2,1)S(1)} collective-permute-done((bf16[4,64,2048]{2,1,0:T(8,128)(2,1)S(1)}, bf16[4,64,2048]{2,1,0:T(8,128)(2,1)S(1)}, u32[]{:S(2)}, u32[]{:S(2)}) %collective-permute-start) | collective-permute-done | bytes 1048608 | tf_op jit(solution)/shard_map/while/body/eval_jaxpr/ppermute | solution.py:26
  103.3 3.4 collective-permute-start.1
  106.7 3.3 collective-permute-start.2
  110.1 5.2 %collective-permute-done.1 = f32[1,64,2048]{2,1,0:T(8,128)S(1)} collective-permute-done((f32[1,64,2048]{2,1,0:T(8,128)S(1)}, f32[1,64,2048]{2,1,0:T(8,128)S(1)}, u32[]{:S(2)}, u32[]{:S(2)}) %collective-permute-start.1) | collective-permute-done | bytes 524320 | tf_op jit(solution)/shard_map/while/body/eval_jaxpr/ppermute | solution.py:15
  115.3 6.1 %collective-permute-done.2 = f32[1,64,2048]{2,1,0:T(8,128)S(1)} collective-permute-done((f32[1,64,2048]{2,1,0:T(8,128)S(1)}, f32[1,64,2048]{2,1,0:T(8,128)S(1)}, u32[]{:S(2)}, u32[]{:S(2)}) %collective-permute-start.2) | collective-permute-done | bytes 524320 | tf_op jit(solution)/shard_map/while/body/eval_jaxpr/ppermute | solution.py:18
  126.7 8.2 %collective-permute-start.4 = (f32[1,64,2048]{2,1,0:T(8,128)}, f32[1,64,2048]{2,1,0:T(8,128)}, u32[]{:S(2)}, u32[]{:S(2)}) collective-permute-start(f32[1,64,2048]{2,1,0:T(8,128)} %get-tuple-element.128), channel_id=1, source_target_pairs={{1,0},{2,1},{3,2},{4,3},{5,4},{6,5},{7,6},{9,8},{10,9},{11,10},{12... | collective-permute-start | bytes 1572872 | tf_op jit(solution)/shard_map/while/body/eval_jaxpr/ppermute | solution.py:18
  136.0 4.6 %collective-permute-done.3 = f32[1,64,2048]{2,1,0:T(8,128)} collective-permute-done((f32[1,64,2048]{2,1,0:T(8,128)}, f32[1,64,2048]{2,1,0:T(8,128)}, u32[]{:S(2)}, u32[]{:S(2)}) %collective-permute-start.3) | collective-permute-done | bytes 524320 | tf_op jit(solution)/shard_map/while/body/eval_jaxpr/ppermute | solution.py:15
  140.5 7.3 %collective-permute-done.4 = f32[1,64,2048]{2,1,0:T(8,128)} collective-permute-done((f32[1,64,2048]{2,1,0:T(8,128)}, f32[1,64,2048]{2,1,0:T(8,128)}, u32[]{:S(2)}, u32[]{:S(2)}) %collective-permute-start.4) | collective-permute-done | bytes 524320 | tf_op jit(solution)/shard_map/while/body/eval_jaxpr/ppermute | solution.py:18
  147.9 11.1 %fusion.40 = f32[4,64,2048]{2,1,0:T(8,128)} fusion(f32[4,64,2048]{2,1,0:T(8,128)} %get-tuple-element.148, f32[4,64,2048]{2,1,0:T(8,128)} %copy-done.2, f32[4,64,1]{2,1,0:T(8,128)S(1)} %get-tuple-element.125, f32[4,64,1]{2,1,0:T(8,128)S(1)} %get-tuple-element.126, f32[1,64,2048]{2,1,0:T(8,128)} %collective-permute-done.3, ...), kind=kLoop, calls=%fused_computation.14.clone.1 | loop fusion | flops 12058624 | bytes 12587009 | tf_op jit(solution)/shard_map/while/body/eval_jaxpr/add | solution.py:117
  160.9 3.6 collective-permute-start
  164.5 12.3 %collective-permute-done = bf16[4,64,2048]{2,1,0:T(8,128)(2,1)S(1)} collective-permute-done((bf16[4,64,2048]{2,1,0:T(8,128)(2,1)S(1)}, bf16[4,64,2048]{2,1,0:T(8,128)(2,1)S(1)}, u32[]{:S(2)}, u32[]{:S(2)}) %collective-permute-start) | collective-permute-done | bytes 1048608 | tf_op jit(solution)/shard_map/while/body/eval_jaxpr/ppermute | solution.py:26
  179.3 4.8 %collective-permute-start.2 = (f32[1,64,2048]{2,1,0:T(8,128)S(1)}, f32[1,64,2048]{2,1,0:T(8,128)S(1)}, u32[]{:S(2)}, u32[]{:S(2)}) collective-permute-start(f32[1,64,2048]{2,1,0:T(8,128)S(1)} %get-tuple-element.124), channel_id=1, source_target_pairs={{1,0},{2,1},{3,2},{4,3},{5,4},{6,5},{7,6},{9,8},{10,9},{11,10},{12... | collective-permute-start | bytes 1572872 | tf_op jit(solution)/shard_map/while/body/eval_jaxpr/ppermute | solution.py:18
  184.2 5.2 %collective-permute-done.1 = f32[1,64,2048]{2,1,0:T(8,128)S(1)} collective-permute-done((f32[1,64,2048]{2,1,0:T(8,128)S(1)}, f32[1,64,2048]{2,1,0:T(8,128)S(1)}, u32[]{:S(2)}, u32[]{:S(2)}) %collective-permute-start.1) | collective-permute-done | bytes 524320 | tf_op jit(solution)/shard_map/while/body/eval_jaxpr/ppermute | solution.py:15
  189.4 14.5 %collective-permute-done.2 = f32[1,64,2048]{2,1,0:T(8,128)S(1)} collective-permute-done((f32[1,64,2048]{2,1,0:T(8,128)S(1)}, f32[1,64,2048]{2,1,0:T(8,128)S(1)}, u32[]{:S(2)}, u32[]{:S(2)}) %collective-permute-start.2) | collective-permute-done | bytes 524320 | tf_op jit(solution)/shard_map/while/body/eval_jaxpr/ppermute | solution.py:18
  209.2 4.8 %collective-permute-start.4 = (f32[1,64,2048]{2,1,0:T(8,128)}, f32[1,64,2048]{2,1,0:T(8,128)}, u32[]{:S(2)}, u32[]{:S(2)}) collective-permute-start(f32[1,64,2048]{2,1,0:T(8,128)} %get-tuple-element.128), channel_id=1, source_target_pairs={{1,0},{2,1},{3,2},{4,3},{5,4},{6,5},{7,6},{9,8},{10,9},{11,10},{12... | collective-permute-start | bytes 1572872 | tf_op jit(solution)/shard_map/while/body/eval_jaxpr/ppermute | solution.py:18
  215.1 4.6 %collective-permute-done.3 = f32[1,64,2048]{2,1,0:T(8,128)} collective-permute-done((f32[1,64,2048]{2,1,0:T(8,128)}, f32[1,64,2048]{2,1,0:T(8,128)}, u32[]{:S(2)}, u32[]{:S(2)}) %collective-permute-start.3) | collective-permute-done | bytes 524320 | tf_op jit(solution)/shard_map/while/body/eval_jaxpr/ppermute | solution.py:15
  219.6 5.5 %collective-permute-done.4 = f32[1,64,2048]{2,1,0:T(8,128)} collective-permute-done((f32[1,64,2048]{2,1,0:T(8,128)}, f32[1,64,2048]{2,1,0:T(8,128)}, u32[]{:S(2)}, u32[]{:S(2)}) %collective-permute-start.4) | collective-permute-done | bytes 524320 | tf_op jit(solution)/shard_map/while/body/eval_jaxpr/ppermute | solution.py:18
  225.1 11.1 %fusion.40 = f32[4,64,2048]{2,1,0:T(8,128)} fusion(f32[4,64,2048]{2,1,0:T(8,128)} %get-tuple-element.148, f32[4,64,2048]{2,1,0:T(8,128)} %copy-done.2, f32[4,64,1]{2,1,0:T(8,128)S(1)} %get-tuple-element.125, f32[4,64,1]{2,1,0:T(8,128)S(1)} %get-tuple-element.126, f32[1,64,2048]{2,1,0:T(8,128)} %collective-permute-done.3, ...), kind=kLoop, calls=%fused_computation.14.clone.1 | loop fusion | flops 12058624 | bytes 12587009 | tf_op jit(solution)/shard_map/while/body/eval_jaxpr/add | solution.py:117
  240.1 12.3 %collective-permute-done = bf16[4,64,2048]{2,1,0:T(8,128)(2,1)S(1)} collective-permute-done((bf16[4,64,2048]{2,1,0:T(8,128)(2,1)S(1)}, bf16[4,64,2048]{2,1,0:T(8,128)(2,1)S(1)}, u32[]{:S(2)}, u32[]{:S(2)}) %collective-permute-start) | collective-permute-done | bytes 1048608 | tf_op jit(solution)/shard_map/while/body/eval_jaxpr/ppermute | solution.py:26
  254.9 4.8 %collective-permute-start.2 = (f32[1,64,2048]{2,1,0:T(8,128)S(1)}, f32[1,64,2048]{2,1,0:T(8,128)S(1)}, u32[]{:S(2)}, u32[]{:S(2)}) collective-permute-start(f32[1,64,2048]{2,1,0:T(8,128)S(1)} %get-tuple-element.124), channel_id=1, source_target_pairs={{1,0},{2,1},{3,2},{4,3},{5,4},{6,5},{7,6},{9,8},{10,9},{11,10},{12... | collective-permute-start | bytes 1572872 | tf_op jit(solution)/shard_map/while/body/eval_jaxpr/ppermute | solution.py:18
  259.8 5.2 %collective-permute-done.1 = f32[1,64,2048]{2,1,0:T(8,128)S(1)} collective-permute-done((f32[1,64,2048]{2,1,0:T(8,128)S(1)}, f32[1,64,2048]{2,1,0:T(8,128)S(1)}, u32[]{:S(2)}, u32[]{:S(2)}) %collective-permute-start.1) | collective-permute-done | bytes 524320 | tf_op jit(solution)/shard_map/while/body/eval_jaxpr/ppermute | solution.py:15
  265.1 6.2 %collective-permute-done.2 = f32[1,64,2048]{2,1,0:T(8,128)S(1)} collective-permute-done((f32[1,64,2048]{2,1,0:T(8,128)S(1)}, f32[1,64,2048]{2,1,0:T(8,128)S(1)}, u32[]{:S(2)}, u32[]{:S(2)}) %collective-permute-start.2) | collective-permute-done | bytes 524320 | tf_op jit(solution)/shard_map/while/body/eval_jaxpr/ppermute | solution.py:18
  276.5 4.8 %collective-permute-start.4 = (f32[1,64,2048]{2,1,0:T(8,128)}, f32[1,64,2048]{2,1,0:T(8,128)}, u32[]{:S(2)}, u32[]{:S(2)}) collective-permute-start(f32[1,64,2048]{2,1,0:T(8,128)} %get-tuple-element.128), channel_id=1, source_target_pairs={{1,0},{2,1},{3,2},{4,3},{5,4},{6,5},{7,6},{9,8},{10,9},{11,10},{12... | collective-permute-start | bytes 1572872 | tf_op jit(solution)/shard_map/while/body/eval_jaxpr/ppermute | solution.py:18
  282.4 4.5 %collective-permute-done.3 = f32[1,64,2048]{2,1,0:T(8,128)} collective-permute-done((f32[1,64,2048]{2,1,0:T(8,128)}, f32[1,64,2048]{2,1,0:T(8,128)}, u32[]{:S(2)}, u32[]{:S(2)}) %collective-permute-start.3) | collective-permute-done | bytes 524320 | tf_op jit(solution)/shard_map/while/body/eval_jaxpr/ppermute | solution.py:15
  286.9 11.0 %collective-permute-done.4 = f32[1,64,2048]{2,1,0:T(8,128)} collective-permute-done((f32[1,64,2048]{2,1,0:T(8,128)}, f32[1,64,2048]{2,1,0:T(8,128)}, u32[]{:S(2)}, u32[]{:S(2)}) %collective-permute-start.4) | collective-permute-done | bytes 524320 | tf_op jit(solution)/shard_map/while/body/eval_jaxpr/ppermute | solution.py:18
  297.9 11.1 %fusion.40 = f32[4,64,2048]{2,1,0:T(8,128)} fusion(f32[4,64,2048]{2,1,0:T(8,128)} %get-tuple-element.148, f32[4,64,2048]{2,1,0:T(8,128)} %copy-done.2, f32[4,64,1]{2,1,0:T(8,128)S(1)} %get-tuple-element.125, f32[4,64,1]{2,1,0:T(8,128)S(1)} %get-tuple-element.126, f32[1,64,2048]{2,1,0:T(8,128)} %collective-permute-done.3, ...), kind=kLoop, calls=%fused_computation.14.clone.1 | loop fusion | flops 12058624 | bytes 12587009 | tf_op jit(solution)/shard_map/while/body/eval_jaxpr/add | solution.py:117
  310.9 4.5 %collective-permute-start = (bf16[4,64,2048]{2,1,0:T(8,128)(2,1)S(1)}, bf16[4,64,2048]{2,1,0:T(8,128)(2,1)S(1)}, u32[]{:S(2)}, u32[]{:S(2)}) collective-permute-start(bf16[4,64,2048]{2,1,0:T(8,128)(2,1)S(1)} %convert_element_type.38), channel_id=1, source_target_pairs={{8,0},{16,8},{24,16},{9,1},{17,9},{25,17},{10,2},{18,10},{26,18},{... | collective-permute-start | bytes 3145736 | tf_op jit(solution)/shard_map/while/body/eval_jaxpr/ppermute | solution.py:26
  315.4 12.3 %collective-permute-done = bf16[4,64,2048]{2,1,0:T(8,128)(2,1)S(1)} collective-permute-done((bf16[4,64,2048]{2,1,0:T(8,128)(2,1)S(1)}, bf16[4,64,2048]{2,1,0:T(8,128)(2,1)S(1)}, u32[]{:S(2)}, u32[]{:S(2)}) %collective-permute-start) | collective-permute-done | bytes 1048608 | tf_op jit(solution)/shard_map/while/body/eval_jaxpr/ppermute | solution.py:26
  330.2 4.8 %collective-permute-start.2 = (f32[1,64,2048]{2,1,0:T(8,128)S(1)}, f32[1,64,2048]{2,1,0:T(8,128)S(1)}, u32[]{:S(2)}, u32[]{:S(2)}) collective-permute-start(f32[1,64,2048]{2,1,0:T(8,128)S(1)} %get-tuple-element.124), channel_id=1, source_target_pairs={{1,0},{2,1},{3,2},{4,3},{5,4},{6,5},{7,6},{9,8},{10,9},{11,10},{12... | collective-permute-start | bytes 1572872 | tf_op jit(solution)/shard_map/while/body/eval_jaxpr/ppermute | solution.py:18
  335.2 5.2 %collective-permute-done.1 = f32[1,64,2048]{2,1,0:T(8,128)S(1)} collective-permute-done((f32[1,64,2048]{2,1,0:T(8,128)S(1)}, f32[1,64,2048]{2,1,0:T(8,128)S(1)}, u32[]{:S(2)}, u32[]{:S(2)}) %collective-permute-start.1) | collective-permute-done | bytes 524320 | tf_op jit(solution)/shard_map/while/body/eval_jaxpr/ppermute | solution.py:15
  340.4 15.4 %collective-permute-done.2 = f32[1,64,2048]{2,1,0:T(8,128)S(1)} collective-permute-done((f32[1,64,2048]{2,1,0:T(8,128)S(1)}, f32[1,64,2048]{2,1,0:T(8,128)S(1)}, u32[]{:S(2)}, u32[]{:S(2)}) %collective-permute-start.2) | collective-permute-done | bytes 524320 | tf_op jit(solution)/shard_map/while/body/eval_jaxpr/ppermute | solution.py:18
  361.0 4.8 %collective-permute-start.4 = (f32[1,64,2048]{2,1,0:T(8,128)}, f32[1,64,2048]{2,1,0:T(8,128)}, u32[]{:S(2)}, u32[]{:S(2)}) collective-permute-start(f32[1,64,2048]{2,1,0:T(8,128)} %get-tuple-element.128), channel_id=1, source_target_pairs={{1,0},{2,1},{3,2},{4,3},{5,4},{6,5},{7,6},{9,8},{10,9},{11,10},{12... | collective-permute-start | bytes 1572872 | tf_op jit(solution)/shard_map/while/body/eval_jaxpr/ppermute | solution.py:18
  366.9 4.6 %collective-permute-done.3 = f32[1,64,2048]{2,1,0:T(8,128)} collective-permute-done((f32[1,64,2048]{2,1,0:T(8,128)}, f32[1,64,2048]{2,1,0:T(8,128)}, u32[]{:S(2)}, u32[]{:S(2)}) %collective-permute-start.3) | collective-permute-done | bytes 524320 | tf_op jit(solution)/shard_map/while/body/eval_jaxpr/ppermute | solution.py:15
  371.5 5.5 %collective-permute-done.4 = f32[1,64,2048]{2,1,0:T(8,128)} collective-permute-done((f32[1,64,2048]{2,1,0:T(8,128)}, f32[1,64,2048]{2,1,0:T(8,128)}, u32[]{:S(2)}, u32[]{:S(2)}) %collective-permute-start.4) | collective-permute-done | bytes 524320 | tf_op jit(solution)/shard_map/while/body/eval_jaxpr/ppermute | solution.py:18
  377.0 11.1 %fusion.40 = f32[4,64,2048]{2,1,0:T(8,128)} fusion(f32[4,64,2048]{2,1,0:T(8,128)} %get-tuple-element.148, f32[4,64,2048]{2,1,0:T(8,128)} %copy-done.2, f32[4,64,1]{2,1,0:T(8,128)S(1)} %get-tuple-element.125, f32[4,64,1]{2,1,0:T(8,128)S(1)} %get-tuple-element.126, f32[1,64,2048]{2,1,0:T(8,128)} %collective-permute-done.3, ...), kind=kLoop, calls=%fused_computation.14.clone.1 | loop fusion | flops 12058624 | bytes 12587009 | tf_op jit(solution)/shard_map/while/body/eval_jaxpr/add | solution.py:117
  (127 shorter events, 70.0 us)
Async XLA Ops:
  0.0 44.1 %copy-start = (bf16[96,128,128]{2,1,0:T(8,128)(2,1)S(1)}, bf16[96,128,128]{2,1,0:T(8,128)(2,1)}, u32[]{:S(2)}) copy-start(bf16[96,128,128]{2,1,0:T(8,128)(2,1)} %param.14) | copy-start | bytes 9437188
  4.3 23.8 %all-to-all-start = ((s32[32,1,6]{2,1,0:T(1,128)}), s32[32,1,6]{2,1,0:T(1,128)S(1)}, u32[]{:S(2)}, u32[]{:S(2)}) async-start(s32[32,1,6]{2,1,0:T(1,128)} %bitcast.3), calls=%async_computation | async-start | bytes 32768 | tf_op jit(solution)/shard_map/all_to_all | solution.py:92
  32.4 16.7 %copy-start.8 = (f32[96,128]{1,0:T(8,128)S(1)}, f32[96,128]{1,0:T(8,128)}, u32[]{:S(2)}) copy-start(f32[96,128]{1,0:T(8,128)} %param.15) | copy-start | bytes 147460
  32.4 16.7 %copy-start.9 = (f32[96,128]{1,0:T(8,128)S(1)}, f32[96,128]{1,0:T(8,128)}, u32[]{:S(2)}) copy-start(f32[96,128]{1,0:T(8,128)} %param.16) | copy-start | bytes 147460
  32.4 16.7 %copy-start.10 = (s32[96,128]{1,0:T(8,128)S(1)}, s32[96,128]{1,0:T(8,128)}, u32[]{:S(2)}) copy-start(s32[96,128]{1,0:T(8,128)} %param.17) | copy-start | bytes 147460
  32.4 11.1 %all-to-all-start.1 = ((f32[32,6,128]{2,1,0:T(8,128)}), f32[32,6,128]{2,1,0:T(8,128)S(1)}, u32[]{:S(2)}, u32[]{:S(2)}) async-start(f32[32,6,128]{2,1,0:T(8,128)} %reshape.60), calls=%async_computation.1 | async-start | bytes 262144 | tf_op jit(solution)/shard_map/all_to_all | solution.py:96
  53.1 10.3 %all-to-all-start.2 = ((f32[32,6,128]{2,1,0:T(8,128)}), f32[32,6,128]{2,1,0:T(8,128)S(1)}, u32[]{:S(2)}, u32[]{:S(2)}) async-start(f32[32,6,128]{2,1,0:T(8,128)} %reshape.62), calls=%async_computation.2 | async-start | bytes 262144 | tf_op jit(solution)/shard_map/all_to_all | solution.py:101
  86.4 16.3 %copy-start.3 = (bf16[4,64,2048]{2,1,0:T(8,128)(2,1)S(1)}, bf16[4,64,2048]{2,1,0:T(8,128)(2,1)}, u32[]{:S(2)}) copy-start(bf16[4,64,2048]{2,1,0:T(8,128)(2,1)} %get-tuple-element.146) | copy-start | bytes 3145732 | tf_op jit(solution)/shard_map/while
  86.4 16.3 %copy-start.5 = (f32[4,64,2048]{2,1,0:T(8,128)S(1)}, f32[4,64,2048]{2,1,0:T(8,128)}, u32[]{:S(2)}) copy-start(f32[4,64,2048]{2,1,0:T(8,128)} %get-tuple-element.147) | copy-start | bytes 6291460 | tf_op jit(solution)/shard_map/while
  88.3 14.4 %collective-permute-start = (bf16[4,64,2048]{2,1,0:T(8,128)(2,1)S(1)}, bf16[4,64,2048]{2,1,0:T(8,128)(2,1)S(1)}, u32[]{:S(2)}, u32[]{:S(2)}) collective-permute-start(bf16[4,64,2048]{2,1,0:T(8,128)(2,1)S(1)} %convert_element_type.38), channel_id=1, source_target_pairs={{8,0},{16,8},{24,16},{9,1},{17,9},{25,17},{10,2},{18,10},{26,18},{... | collective-permute-start | bytes 3145736 | tf_op jit(solution)/shard_map/while/body/eval_jaxpr/ppermute | solution.py:26
  102.6 18.8 %copy-start.4 = (bf16[4,64,2048]{2,1,0:T(8,128)(2,1)}, bf16[4,64,2048]{2,1,0:T(8,128)(2,1)S(1)}, u32[]{:S(2)}) copy-start(bf16[4,64,2048]{2,1,0:T(8,128)(2,1)S(1)} %collective-permute-done) | copy-start | bytes 3145732 | tf_op jit(solution)/shard_map/while
  103.1 19.9 %copy-start.1 = (f32[4,64,2048]{2,1,0:T(8,128)}, f32[4,64,2048]{2,1,0:T(8,128)S(1)}, u32[]{:S(2)}) copy-start(f32[4,64,2048]{2,1,0:T(8,128)S(1)} %convert_multiply_fusion.2) | copy-start | bytes 6291460 | tf_op jit(solution)/shard_map/while
  103.3 12.1 %collective-permute-start.1 = (f32[1,64,2048]{2,1,0:T(8,128)S(1)}, f32[1,64,2048]{2,1,0:T(8,128)S(1)}, u32[]{:S(2)}, u32[]{:S(2)}) collective-permute-start(f32[1,64,2048]{2,1,0:T(8,128)S(1)} %get-tuple-element.123), channel_id=1, source_target_pairs={{0,1},{1,2},{2,3},{3,4},{4,5},{5,6},{6,7},{8,9},{9,10},{10,11},{11... | collective-permute-start | bytes 1572872 | tf_op jit(solution)/shard_map/while/body/eval_jaxpr/ppermute | solution.py:15
  106.7 14.8 %collective-permute-start.2 = (f32[1,64,2048]{2,1,0:T(8,128)S(1)}, f32[1,64,2048]{2,1,0:T(8,128)S(1)}, u32[]{:S(2)}, u32[]{:S(2)}) collective-permute-start(f32[1,64,2048]{2,1,0:T(8,128)S(1)} %get-tuple-element.124), channel_id=1, source_target_pairs={{1,0},{2,1},{3,2},{4,3},{5,4},{6,5},{7,6},{9,8},{10,9},{11,10},{12... | collective-permute-start | bytes 1572872 | tf_op jit(solution)/shard_map/while/body/eval_jaxpr/ppermute | solution.py:18
  115.3 7.7 %copy-start.6 = (f32[1,64,2048]{2,1,0:T(8,128)}, f32[1,64,2048]{2,1,0:T(8,128)S(1)}, u32[]{:S(2)}) copy-start(f32[1,64,2048]{2,1,0:T(8,128)S(1)} %collective-permute-done.1) | copy-start | bytes 1572868 | tf_op jit(solution)/shard_map/while
  123.1 1.7 copy-start.2
  124.7 15.8 %collective-permute-start.3 = (f32[1,64,2048]{2,1,0:T(8,128)}, f32[1,64,2048]{2,1,0:T(8,128)}, u32[]{:S(2)}, u32[]{:S(2)}) collective-permute-start(f32[1,64,2048]{2,1,0:T(8,128)} %get-tuple-element.127), channel_id=1, source_target_pairs={{0,1},{1,2},{2,3},{3,4},{4,5},{5,6},{6,7},{8,9},{9,10},{10,11},{11... | collective-permute-start | bytes 1572872 | tf_op jit(solution)/shard_map/while/body/eval_jaxpr/ppermute | solution.py:15
  126.7 21.2 %collective-permute-start.4 = (f32[1,64,2048]{2,1,0:T(8,128)}, f32[1,64,2048]{2,1,0:T(8,128)}, u32[]{:S(2)}, u32[]{:S(2)}) collective-permute-start(f32[1,64,2048]{2,1,0:T(8,128)} %get-tuple-element.128), channel_id=1, source_target_pairs={{1,0},{2,1},{3,2},{4,3},{5,4},{6,5},{7,6},{9,8},{10,9},{11,10},{12... | collective-permute-start | bytes 1572872 | tf_op jit(solution)/shard_map/while/body/eval_jaxpr/ppermute | solution.py:18
  159.0 17.8 %copy-start.3 = (bf16[4,64,2048]{2,1,0:T(8,128)(2,1)S(1)}, bf16[4,64,2048]{2,1,0:T(8,128)(2,1)}, u32[]{:S(2)}) copy-start(bf16[4,64,2048]{2,1,0:T(8,128)(2,1)} %get-tuple-element.146) | copy-start | bytes 3145732 | tf_op jit(solution)/shard_map/while
  159.0 17.8 %copy-start.5 = (f32[4,64,2048]{2,1,0:T(8,128)S(1)}, f32[4,64,2048]{2,1,0:T(8,128)}, u32[]{:S(2)}) copy-start(f32[4,64,2048]{2,1,0:T(8,128)} %get-tuple-element.147) | copy-start | bytes 6291460 | tf_op jit(solution)/shard_map/while
  160.9 15.9 %collective-permute-start = (bf16[4,64,2048]{2,1,0:T(8,128)(2,1)S(1)}, bf16[4,64,2048]{2,1,0:T(8,128)(2,1)S(1)}, u32[]{:S(2)}, u32[]{:S(2)}) collective-permute-start(bf16[4,64,2048]{2,1,0:T(8,128)(2,1)S(1)} %convert_element_type.38), channel_id=1, source_target_pairs={{8,0},{16,8},{24,16},{9,1},{17,9},{25,17},{10,2},{18,10},{26,18},{... | collective-permute-start | bytes 3145736 | tf_op jit(solution)/shard_map/while/body/eval_jaxpr/ppermute | solution.py:26
  176.8 27.2 %copy-start.4 = (bf16[4,64,2048]{2,1,0:T(8,128)(2,1)}, bf16[4,64,2048]{2,1,0:T(8,128)(2,1)S(1)}, u32[]{:S(2)}) copy-start(bf16[4,64,2048]{2,1,0:T(8,128)(2,1)S(1)} %collective-permute-done) | copy-start | bytes 3145732 | tf_op jit(solution)/shard_map/while
  177.3 28.3 %copy-start.1 = (f32[4,64,2048]{2,1,0:T(8,128)}, f32[4,64,2048]{2,1,0:T(8,128)S(1)}, u32[]{:S(2)}) copy-start(f32[4,64,2048]{2,1,0:T(8,128)S(1)} %convert_multiply_fusion.2) | copy-start | bytes 6291460 | tf_op jit(solution)/shard_map/while
  177.4 12.1 %collective-permute-start.1 = (f32[1,64,2048]{2,1,0:T(8,128)S(1)}, f32[1,64,2048]{2,1,0:T(8,128)S(1)}, u32[]{:S(2)}, u32[]{:S(2)}) collective-permute-start(f32[1,64,2048]{2,1,0:T(8,128)S(1)} %get-tuple-element.123), channel_id=1, source_target_pairs={{0,1},{1,2},{2,3},{3,4},{4,5},{5,6},{6,7},{8,9},{9,10},{10,11},{11... | collective-permute-start | bytes 1572872 | tf_op jit(solution)/shard_map/while/body/eval_jaxpr/ppermute | solution.py:15
  179.3 24.6 %collective-permute-start.2 = (f32[1,64,2048]{2,1,0:T(8,128)S(1)}, f32[1,64,2048]{2,1,0:T(8,128)S(1)}, u32[]{:S(2)}, u32[]{:S(2)}) collective-permute-start(f32[1,64,2048]{2,1,0:T(8,128)S(1)} %get-tuple-element.124), channel_id=1, source_target_pairs={{1,0},{2,1},{3,2},{4,3},{5,4},{6,5},{7,6},{9,8},{10,9},{11,10},{12... | collective-permute-start | bytes 1572872 | tf_op jit(solution)/shard_map/while/body/eval_jaxpr/ppermute | solution.py:18
  189.4 16.1 %copy-start.6 = (f32[1,64,2048]{2,1,0:T(8,128)}, f32[1,64,2048]{2,1,0:T(8,128)S(1)}, u32[]{:S(2)}) copy-start(f32[1,64,2048]{2,1,0:T(8,128)S(1)} %collective-permute-done.1) | copy-start | bytes 1572868 | tf_op jit(solution)/shard_map/while
  207.2 12.4 %collective-permute-start.3 = (f32[1,64,2048]{2,1,0:T(8,128)}, f32[1,64,2048]{2,1,0:T(8,128)}, u32[]{:S(2)}, u32[]{:S(2)}) collective-permute-start(f32[1,64,2048]{2,1,0:T(8,128)} %get-tuple-element.127), channel_id=1, source_target_pairs={{0,1},{1,2},{2,3},{3,4},{4,5},{5,6},{6,7},{8,9},{9,10},{10,11},{11... | collective-permute-start | bytes 1572872 | tf_op jit(solution)/shard_map/while/body/eval_jaxpr/ppermute | solution.py:15
  209.2 16.0 %collective-permute-start.4 = (f32[1,64,2048]{2,1,0:T(8,128)}, f32[1,64,2048]{2,1,0:T(8,128)}, u32[]{:S(2)}, u32[]{:S(2)}) collective-permute-start(f32[1,64,2048]{2,1,0:T(8,128)} %get-tuple-element.128), channel_id=1, source_target_pairs={{1,0},{2,1},{3,2},{4,3},{5,4},{6,5},{7,6},{9,8},{10,9},{11,10},{12... | collective-permute-start | bytes 1572872 | tf_op jit(solution)/shard_map/while/body/eval_jaxpr/ppermute | solution.py:18
  236.2 16.1 %copy-start.3 = (bf16[4,64,2048]{2,1,0:T(8,128)(2,1)S(1)}, bf16[4,64,2048]{2,1,0:T(8,128)(2,1)}, u32[]{:S(2)}) copy-start(bf16[4,64,2048]{2,1,0:T(8,128)(2,1)} %get-tuple-element.146) | copy-start | bytes 3145732 | tf_op jit(solution)/shard_map/while
  236.2 16.1 %copy-start.5 = (f32[4,64,2048]{2,1,0:T(8,128)S(1)}, f32[4,64,2048]{2,1,0:T(8,128)}, u32[]{:S(2)}) copy-start(f32[4,64,2048]{2,1,0:T(8,128)} %get-tuple-element.147) | copy-start | bytes 6291460 | tf_op jit(solution)/shard_map/while
  238.1 14.2 %collective-permute-start = (bf16[4,64,2048]{2,1,0:T(8,128)(2,1)S(1)}, bf16[4,64,2048]{2,1,0:T(8,128)(2,1)S(1)}, u32[]{:S(2)}, u32[]{:S(2)}) collective-permute-start(bf16[4,64,2048]{2,1,0:T(8,128)(2,1)S(1)} %convert_element_type.38), channel_id=1, source_target_pairs={{8,0},{16,8},{24,16},{9,1},{17,9},{25,17},{10,2},{18,10},{26,18},{... | collective-permute-start | bytes 3145736 | tf_op jit(solution)/shard_map/while/body/eval_jaxpr/ppermute | solution.py:26
  252.4 18.9 %copy-start.4 = (bf16[4,64,2048]{2,1,0:T(8,128)(2,1)}, bf16[4,64,2048]{2,1,0:T(8,128)(2,1)S(1)}, u32[]{:S(2)}) copy-start(bf16[4,64,2048]{2,1,0:T(8,128)(2,1)S(1)} %collective-permute-done) | copy-start | bytes 3145732 | tf_op jit(solution)/shard_map/while
  252.9 20.0 %copy-start.1 = (f32[4,64,2048]{2,1,0:T(8,128)}, f32[4,64,2048]{2,1,0:T(8,128)S(1)}, u32[]{:S(2)}) copy-start(f32[4,64,2048]{2,1,0:T(8,128)S(1)} %convert_multiply_fusion.2) | copy-start | bytes 6291460 | tf_op jit(solution)/shard_map/while
  253.0 12.1 %collective-permute-start.1 = (f32[1,64,2048]{2,1,0:T(8,128)S(1)}, f32[1,64,2048]{2,1,0:T(8,128)S(1)}, u32[]{:S(2)}, u32[]{:S(2)}) collective-permute-start(f32[1,64,2048]{2,1,0:T(8,128)S(1)} %get-tuple-element.123), channel_id=1, source_target_pairs={{0,1},{1,2},{2,3},{3,4},{4,5},{5,6},{6,7},{8,9},{9,10},{10,11},{11... | collective-permute-start | bytes 1572872 | tf_op jit(solution)/shard_map/while/body/eval_jaxpr/ppermute | solution.py:15
  254.9 16.4 %collective-permute-start.2 = (f32[1,64,2048]{2,1,0:T(8,128)S(1)}, f32[1,64,2048]{2,1,0:T(8,128)S(1)}, u32[]{:S(2)}, u32[]{:S(2)}) collective-permute-start(f32[1,64,2048]{2,1,0:T(8,128)S(1)} %get-tuple-element.124), channel_id=1, source_target_pairs={{1,0},{2,1},{3,2},{4,3},{5,4},{6,5},{7,6},{9,8},{10,9},{11,10},{12... | collective-permute-start | bytes 1572872 | tf_op jit(solution)/shard_map/while/body/eval_jaxpr/ppermute | solution.py:18
  265.1 7.9 %copy-start.6 = (f32[1,64,2048]{2,1,0:T(8,128)}, f32[1,64,2048]{2,1,0:T(8,128)S(1)}, u32[]{:S(2)}) copy-start(f32[1,64,2048]{2,1,0:T(8,128)S(1)} %collective-permute-done.1) | copy-start | bytes 1572868 | tf_op jit(solution)/shard_map/while
  274.6 12.3 %collective-permute-start.3 = (f32[1,64,2048]{2,1,0:T(8,128)}, f32[1,64,2048]{2,1,0:T(8,128)}, u32[]{:S(2)}, u32[]{:S(2)}) collective-permute-start(f32[1,64,2048]{2,1,0:T(8,128)} %get-tuple-element.127), channel_id=1, source_target_pairs={{0,1},{1,2},{2,3},{3,4},{4,5},{5,6},{6,7},{8,9},{9,10},{10,11},{11... | collective-permute-start | bytes 1572872 | tf_op jit(solution)/shard_map/while/body/eval_jaxpr/ppermute | solution.py:15
  276.5 21.4 %collective-permute-start.4 = (f32[1,64,2048]{2,1,0:T(8,128)}, f32[1,64,2048]{2,1,0:T(8,128)}, u32[]{:S(2)}, u32[]{:S(2)}) collective-permute-start(f32[1,64,2048]{2,1,0:T(8,128)} %get-tuple-element.128), channel_id=1, source_target_pairs={{1,0},{2,1},{3,2},{4,3},{5,4},{6,5},{7,6},{9,8},{10,9},{11,10},{12... | collective-permute-start | bytes 1572872 | tf_op jit(solution)/shard_map/while/body/eval_jaxpr/ppermute | solution.py:18
  309.0 18.7 %copy-start.3 = (bf16[4,64,2048]{2,1,0:T(8,128)(2,1)S(1)}, bf16[4,64,2048]{2,1,0:T(8,128)(2,1)}, u32[]{:S(2)}) copy-start(bf16[4,64,2048]{2,1,0:T(8,128)(2,1)} %get-tuple-element.146) | copy-start | bytes 3145732 | tf_op jit(solution)/shard_map/while
  309.0 18.7 %copy-start.5 = (f32[4,64,2048]{2,1,0:T(8,128)S(1)}, f32[4,64,2048]{2,1,0:T(8,128)}, u32[]{:S(2)}) copy-start(f32[4,64,2048]{2,1,0:T(8,128)} %get-tuple-element.147) | copy-start | bytes 6291460 | tf_op jit(solution)/shard_map/while
  310.9 16.8 %collective-permute-start = (bf16[4,64,2048]{2,1,0:T(8,128)(2,1)S(1)}, bf16[4,64,2048]{2,1,0:T(8,128)(2,1)S(1)}, u32[]{:S(2)}, u32[]{:S(2)}) collective-permute-start(bf16[4,64,2048]{2,1,0:T(8,128)(2,1)S(1)} %convert_element_type.38), channel_id=1, source_target_pairs={{8,0},{16,8},{24,16},{9,1},{17,9},{25,17},{10,2},{18,10},{26,18},{... | collective-permute-start | bytes 3145736 | tf_op jit(solution)/shard_map/while/body/eval_jaxpr/ppermute | solution.py:26
  327.7 28.1 %copy-start.4 = (bf16[4,64,2048]{2,1,0:T(8,128)(2,1)}, bf16[4,64,2048]{2,1,0:T(8,128)(2,1)S(1)}, u32[]{:S(2)}) copy-start(bf16[4,64,2048]{2,1,0:T(8,128)(2,1)S(1)} %collective-permute-done) | copy-start | bytes 3145732 | tf_op jit(solution)/shard_map/while
  328.2 29.2 %copy-start.1 = (f32[4,64,2048]{2,1,0:T(8,128)}, f32[4,64,2048]{2,1,0:T(8,128)S(1)}, u32[]{:S(2)}) copy-start(f32[4,64,2048]{2,1,0:T(8,128)S(1)} %convert_multiply_fusion.2) | copy-start | bytes 6291460 | tf_op jit(solution)/shard_map/while
  328.3 12.1 %collective-permute-start.1 = (f32[1,64,2048]{2,1,0:T(8,128)S(1)}, f32[1,64,2048]{2,1,0:T(8,128)S(1)}, u32[]{:S(2)}, u32[]{:S(2)}) collective-permute-start(f32[1,64,2048]{2,1,0:T(8,128)S(1)} %get-tuple-element.123), channel_id=1, source_target_pairs={{0,1},{1,2},{2,3},{3,4},{4,5},{5,6},{6,7},{8,9},{9,10},{10,11},{11... | collective-permute-start | bytes 1572872 | tf_op jit(solution)/shard_map/while/body/eval_jaxpr/ppermute | solution.py:15
  330.2 25.5 %collective-permute-start.2 = (f32[1,64,2048]{2,1,0:T(8,128)S(1)}, f32[1,64,2048]{2,1,0:T(8,128)S(1)}, u32[]{:S(2)}, u32[]{:S(2)}) collective-permute-start(f32[1,64,2048]{2,1,0:T(8,128)S(1)} %get-tuple-element.124), channel_id=1, source_target_pairs={{1,0},{2,1},{3,2},{4,3},{5,4},{6,5},{7,6},{9,8},{10,9},{11,10},{12... | collective-permute-start | bytes 1572872 | tf_op jit(solution)/shard_map/while/body/eval_jaxpr/ppermute | solution.py:18
  340.4 17.0 %copy-start.6 = (f32[1,64,2048]{2,1,0:T(8,128)}, f32[1,64,2048]{2,1,0:T(8,128)S(1)}, u32[]{:S(2)}) copy-start(f32[1,64,2048]{2,1,0:T(8,128)S(1)} %collective-permute-done.1) | copy-start | bytes 1572868 | tf_op jit(solution)/shard_map/while
  359.1 12.4 %collective-permute-start.3 = (f32[1,64,2048]{2,1,0:T(8,128)}, f32[1,64,2048]{2,1,0:T(8,128)}, u32[]{:S(2)}, u32[]{:S(2)}) collective-permute-start(f32[1,64,2048]{2,1,0:T(8,128)} %get-tuple-element.127), channel_id=1, source_target_pairs={{0,1},{1,2},{2,3},{3,4},{4,5},{5,6},{6,7},{8,9},{9,10},{10,11},{11... | collective-permute-start | bytes 1572872 | tf_op jit(solution)/shard_map/while/body/eval_jaxpr/ppermute | solution.py:15
  361.0 16.0 %collective-permute-start.4 = (f32[1,64,2048]{2,1,0:T(8,128)}, f32[1,64,2048]{2,1,0:T(8,128)}, u32[]{:S(2)}, u32[]{:S(2)}) collective-permute-start(f32[1,64,2048]{2,1,0:T(8,128)} %get-tuple-element.128), channel_id=1, source_target_pairs={{1,0},{2,1},{3,2},{4,3},{5,4},{6,5},{7,6},{9,8},{10,9},{11,10},{12... | collective-permute-start | bytes 1572872 | tf_op jit(solution)/shard_map/while/body/eval_jaxpr/ppermute | solution.py:18
  (7 other events, 11.5 us)
where the time goes:
time: 391 us; the launch traced here: 388 us
  waiting for transfers between devices  170 us (43%)
  starting transfers between devices  86.2 us (22%)
  other arithmetic  66.2 us (17%)
  local copies, waits for them, and re-layouts  57.3 us (15%)
  matrix products  7.49 us (2%)
    ppermute x8, waiting for transfers between devices, extended(): lax.ppermute(lax.slice_in_dim(block, 0, width, axis=dim), axis, backward)  71.6 us
    ppermute x4, waiting for transfers between devices, passed_along(): return lax.ppermute(block, axis, route)  49.2 us
    add x4, other arithmetic, advance(): return forcing + propagate(incoming, coeff_own)  44.3 us
    ppermute x8, starting transfers between devices, extended(): lax.ppermute(lax.slice_in_dim(block, 0, width, axis=dim), axis, backward)  40.5 us
    ppermute x8, waiting for transfers between devices, extended(): lax.ppermute(lax.slice_in_dim(block, block.shape[dim] - width, None, axis...  39 us
    ppermute x8, starting transfers between devices, extended(): lax.ppermute(lax.slice_in_dim(block, block.shape[dim] - width, None, axis...  16.8 us
    ppermute x4, starting transfers between devices, passed_along(): return lax.ppermute(block, axis, route)  12.1 us
    unnamed x11, local copies, waits for them, and re-layouts  11.5 us
  transfers between devices with their start and end apart: 23, of which 22 were waited for; matrix products, arithmetic and copies ran while one was open for 6% of the time, Pallas kernels for 0%

commit v1 on v0

v1 whole, which is shorter than its diff:
```python
import functools

import jax
import jax.numpy as jnp
from jax import lax
from jax.experimental import pallas as pl
from jax.experimental.pallas import tpu as pltpu
from jax.sharding import PartitionSpec as P

TW = 2
SUB = 2
LANES = 128
PAD = 8
CHUNK = 16
MESH = pl.DeviceIdType.MESH
VMEM = pl.BlockSpec(memory_space=pltpu.VMEM)
SMEM = pl.BlockSpec(memory_space=pltpu.SMEM)


def route_kernel(slots, owner_ref, tile_ref, ids_ref, slot_ref, count_ref):
    devices = ids_ref.shape[0]

    def clear(d, carry):
        count_ref[d] = 0
        for s in range(slots):
            ids_ref[d, s] = 0
        return carry

    lax.fori_loop(0, devices, clear, 0)

    def place(k, carry):
        target = owner_ref[k]
        rank = count_ref[target]
        count_ref[target] = rank + 1
        ids_ref[target, rank] = tile_ref[k]
        slot_ref[k] = target * PAD + rank
        return carry

    lax.fori_loop(0, owner_ref.shape[0], place, 0)


def route(owner, tile, devices, slots):
    return pl.pallas_call(
        functools.partial(route_kernel, slots),
        out_shape=(
            jax.ShapeDtypeStruct((devices, LANES), jnp.int32),
            jax.ShapeDtypeStruct(owner.shape, jnp.int32),
        ),
        in_specs=[SMEM, SMEM],
        out_specs=(SMEM, SMEM),
        scratch_shapes=[pltpu.SMEM((devices,), jnp.int32)],
        name="route",
    )(owner, tile)


def exchange_kernel(count, lat, x_ref, out_ref, send_sem, recv_sem, own_sem):
    me = lax.axis_index("tm") * lat + lax.axis_index("lat")
    barrier = pltpu.get_barrier_semaphore()

    def greet(j, carry):
        to = lax.rem(me + j, count)
        pl.semaphore_signal(barrier, inc=1, device_id=(to // lat, lax.rem(to, lat)), device_id_type=MESH)
        return carry

    lax.fori_loop(1, count, greet, 0)
    own = pltpu.make_async_copy(x_ref.at[me], out_ref.at[me], own_sem)
    own.start()
    pl.semaphore_wait(barrier, count - 1)

    def outgoing(j):
        to = lax.rem(me + j, count)
        return pltpu.make_async_remote_copy(
            src_ref=x_ref.at[to],
            dst_ref=out_ref.at[me],
            send_sem=send_sem.at[j],
            recv_sem=recv_sem.at[j],
            device_id=(to // lat, lax.rem(to, lat)),
            device_id_type=MESH,
        )

    def incoming(j):
        source = lax.rem(me + count - j, count)
        return pltpu.make_async_remote_copy(
            src_ref=x_ref.at[source],
            dst_ref=out_ref.at[source],
            send_sem=send_sem.at[j],
            recv_sem=recv_sem.at[j],
            device_id=(source // lat, lax.rem(source, lat)),
            device_id_type=MESH,
        )

    def launch(j, carry):
        outgoing(j).start()
        return carry

    def land(j, carry):
        incoming(j).wait_recv()
        outgoing(j).wait_send()
        return carry

    lax.fori_loop(1, count, launch, 0)
    own.wait()
    lax.fori_loop(1, count, land, 0)


def exchange(x, collective_id):
    lat = lax.axis_size("lat")
    count = lax.axis_size("tm") * lat
    return pl.pallas_call(
        functools.partial(exchange_kernel, count, lat),
        out_shape=jax.ShapeDtypeStruct(x.shape, x.dtype),
        in_specs=[VMEM],
        out_specs=VMEM,
        scratch_shapes=[
            pltpu.SemaphoreType.DMA((count,)),
            pltpu.SemaphoreType.DMA((count,)),
            pltpu.SemaphoreType.DMA,
        ],
        compiler_params=pltpu.CompilerParams(collective_id=collective_id, has_side_effects=True),
        name="exchange%d" % collective_id,
    )(x)


def tile_place(tile, per_row):
    row = tile // per_row
    lon = (tile - row * per_row) * TW
    column = lon // LANES
    return row, pl.multiple_of(column * LANES, LANES), lon - column * LANES


def gather_kernel(slots, ids_ref, traj_ref, out_ref):
    _, _, levels, nlon = traj_ref.shape
    per_row = nlon // TW
    tile_len = levels * TW
    entry = lax.broadcasted_iota(jnp.int32, (levels, tile_len), 1)
    level = lax.broadcasted_iota(jnp.int32, (levels, tile_len), 0)
    part = lax.rem(entry, TW)
    keep = entry // TW == level
    zeros = jnp.zeros((PAD - slots, tile_len), jnp.float32)

    def one(d, carry):
        rows = []
        for s in range(slots):
            row, start, offset = tile_place(ids_ref[d, s], per_row)
            field = traj_ref[0, row, :, pl.ds(start, LANES)]
            picked = jnp.take_along_axis(field, part + offset, axis=1)
            rows.append(jnp.sum(jnp.where(keep, picked, 0.0), axis=0, keepdims=True))
        out_ref[d] = jnp.concatenate(rows + [zeros], axis=0)
        return carry

    lax.fori_loop(0, out_ref.shape[0], one, 0)


def gather(ids, traj, slots):
    devices = ids.shape[0]
    tile_len = traj.shape[2] * TW
    return pl.pallas_call(
        functools.partial(gather_kernel, slots),
        out_shape=jax.ShapeDtypeStruct((devices, PAD, tile_len), jnp.float32),
        in_specs=[SMEM, VMEM],
        out_specs=VMEM,
        name="gather",
    )(ids, traj)


def split(x):
    top = x.astype(jnp.bfloat16)
    rest = (x - top.astype(jnp.float32)).astype(jnp.bfloat16)
    return jnp.concatenate([top, rest], axis=0)


def blocks_kernel(slot_ref, state_ref, jac_ref, value_ref, weight_ref, valid_ref, out_ref):
    group = PAD
    blocks, _, tile_len = jac_ref.shape
    out_ref[...] = jnp.zeros_like(out_ref)
    rank = lax.rem(lax.broadcasted_iota(jnp.int32, (2 * group, tile_len), 0), group)

    def product(vectors, first, dims):
        both = split(vectors)
        picked = jnp.zeros((2 * group, tile_len), jnp.float32)
        for i in range(group):
            full = lax.dot_general(both, jac_ref[first + i], dims, preferred_element_type=jnp.float32)
            picked = jnp.where(rank == i, full, picked)
        return picked[:group] + picked[group:]

    def one(g, carry):
        first = pl.multiple_of(g * group, group)
        places = [slot_ref[first + i] for i in range(group)]
        states = jnp.concatenate([state_ref[pl.ds(p, 1), :] for p in places], axis=0)
        here = pl.ds(first, group)
        pred = product(states, first, (((1,), (1,)), ((), ())))
        weight = weight_ref[here, :] * valid_ref[here, :].astype(jnp.float32)
        terms = product(weight * (value_ref[here, :] - pred), first, (((1,), (0,)), ((), ())))
        for i, p in enumerate(places):
            out_ref[pl.ds(p, 1), :] = terms[i : i + 1]
        return carry

    lax.fori_loop(0, blocks // group, one, 0)


def block_terms(slot, states, jac, value, weight, valid):
    return pl.pallas_call(
        blocks_kernel,
        out_shape=jax.ShapeDtypeStruct(states.shape, jnp.float32),
        in_specs=[SMEM] + [VMEM] * 5,
        out_specs=VMEM,
        name="blocks",
    )(slot, states, jac, value, weight, valid)


def scatter_kernel(slots, ids_ref, terms_ref, out_ref):
    _, levels, nlon = out_ref.shape
    per_row = nlon // TW
    out_ref[...] = jnp.zeros_like(out_ref)
    lane = lax.broadcasted_iota(jnp.int32, (levels, LANES), 1)
    level = lax.broadcasted_iota(jnp.int32, (levels, LANES), 0)
    source = level * TW + lax.rem(lane, TW)
    owner = lane // TW

    def one(d, carry):
        for s in range(slots):
            row, start, offset = tile_place(ids_ref[d, s], per_row)
            spread = jnp.broadcast_to(terms_ref[d, s : s + 1, :], (levels, levels * TW))
            moved = jnp.take_along_axis(spread, source, axis=1)
            here = (row, slice(None), pl.ds(start, LANES))
            out_ref[here] = out_ref[here] + jnp.where(owner == offset // TW, moved, 0.0)
        return carry

    lax.fori_loop(0, terms_ref.shape[0], one, 0)


def scatter(ids, terms, shape, slots):
    return pl.pallas_call(
        functools.partial(scatter_kernel, slots),
        out_shape=jax.ShapeDtypeStruct(shape, jnp.float32),
        in_specs=[SMEM, VMEM],
        out_specs=VMEM,
        name="scatter",
    )(ids, terms)


def chain_kernel(
    sections, lats, coeff_ref, low_ref, high_ref, end_ref, forcing_ref, out_ref,
    main, low, high, ahead, first_buf, second_buf,
    main_send, main_recv, down_send, up_send, low_recv, high_recv,
):
    section, band = lax.axis_index("tm"), lax.axis_index("lat")
    rows, levels, nlon = end_ref.shape
    chunks = levels // CHUNK
    is_last = section == sections - 1
    has_before, has_low, has_high = section > 0, band > 0, band < lats - 1

    barrier = pltpu.get_barrier_semaphore()
    sides = (
        (jnp.logical_not(is_last), section + 1, band),
        (has_before, section - 1, band),
        (has_low, section, band - 1),
        (has_high, section, band + 1),
    )
    for there, tm, lat in sides:
        @pl.when(there)
        def _(tm=tm, lat=lat):
            pl.semaphore_signal(barrier, inc=1, device_id=(tm, lat), device_id_type=MESH)
    pl.semaphore_wait(barrier, sum(there.astype(jnp.int32) for there, _, _ in sides))

    def remote(src, dst, send, recv, tm, lat):
        return pltpu.make_async_remote_copy(
            src_ref=src, dst_ref=dst, send_sem=send, recv_sem=recv, device_id=(tm, lat), device_id_type=MESH
        )

    def local_main(c):
        return pltpu.make_async_copy(
            end_ref.at[:, pl.ds(pl.multiple_of(c * CHUNK, CHUNK), CHUNK), :], main.at[c], main_recv.at[c]
        )

    def handed(c):
        return remote(ahead.at[c], main.at[c], main_send.at[c], main_recv.at[c], section - 1, band)

    def downward(c):
        return remote(main.at[c, pl.ds(0, SUB)], high.at[c], down_send.at[c], high_recv.at[c], section, band - 1)

    def upward(c):
        return remote(main.at[c, pl.ds(rows - SUB, SUB)], low.at[c], up_send.at[c], low_recv.at[c], section, band + 1)

    @pl.when(jnp.logical_not(has_low))
    def _():
        low[...] = jnp.zeros_like(low)

    @pl.when(jnp.logical_not(has_high))
    def _():
        high[...] = jnp.zeros_like(high)

    @pl.when(is_last)
    def _():
        for c in range(chunks):
            local_main(c).start()

    def pass_edges(c):
        @pl.when(is_last)
        def _():
            local_main(c).wait()

        @pl.when(jnp.logical_not(is_last))
        def _():
            handed(c).wait_recv()

        @pl.when(has_low)
        def _():
            downward(c).start()

        @pl.when(has_high)
        def _():
            upward(c).start()

    def compute(c):
        span = pl.ds(pl.multiple_of(c * CHUNK, CHUNK), CHUNK)
        total = rows + 2 * SUB

        def field(i):
            if i < SUB:
                return low[c, i].astype(jnp.float32)
            if i < SUB + rows:
                return main[c, i - SUB].astype(jnp.float32)
            return high[c, i - SUB - rows].astype(jnp.float32)

        def coeff(i):
            if i < SUB:
                return low_ref[i, span, :].astype(jnp.float32)
            if i < SUB + rows:
                return coeff_ref[0, i - SUB, span, :]
            return high_ref[i - SUB - rows, span, :].astype(jnp.float32)

        def spread(buf, i):
            mid = buf[i]
            return buf[i + 1] + buf[i - 1] + pltpu.roll(mid, 1, 1) + pltpu.roll(mid, nlon - 1, 1) - 4.0 * mid

        for i in range(total):
            first_buf[i] = coeff(i) * field(i)
        for i in range(1, total - 1):
            value = field(i) + spread(first_buf, i)
            second_buf[i] = coeff(i) * value
            if SUB <= i < SUB + rows:
                out_ref[0, i - SUB, span, :] = forcing_ref[i - SUB, span, :] + value
        for r in range(rows):
            value = out_ref[0, r, span, :] + spread(second_buf, r + SUB)
            out_ref[0, r, span, :] = value
            ahead[c, r] = value.astype(jnp.bfloat16)

    pass_edges(0)

    def step(c, carry):
        @pl.when(c + 1 < chunks)
        def _():
            pass_edges(c + 1)

        @pl.when(has_low)
        def _():
            upward(c).wait_recv()

        @pl.when(has_high)
        def _():
            downward(c).wait_recv()

        compute(c)

        @pl.when(has_before)
        def _():
            handed(c).start()

        return carry

    lax.fori_loop(0, chunks, step, 0)

    def finish(c, carry):
        @pl.when(has_low)
        def _():
            downward(c).wait_send()

        @pl.when(has_high)
        def _():
            upward(c).wait_send()

        @pl.when(has_before)
        def _():
            handed(c).wait_send()

        return carry

    lax.fori_loop(0, chunks, finish, 0)


def chain(coeff, low, high, end, forcing):
    rows, levels, nlon = end.shape
    chunks = levels // CHUNK
    part = lambda n, kind: pltpu.VMEM((chunks, n, CHUNK, nlon), kind)
    whole = pltpu.VMEM((rows + 2 * SUB, CHUNK, nlon), jnp.float32)
    return pl.pallas_call(
        functools.partial(chain_kernel, lax.axis_size("tm"), lax.axis_size("lat")),
        out_shape=jax.ShapeDtypeStruct(coeff.shape, jnp.float32),
        in_specs=[VMEM] * 5,
        out_specs=VMEM,
        scratch_shapes=[
            part(rows, jnp.bfloat16),
            part(SUB, jnp.bfloat16),
            part(SUB, jnp.bfloat16),
            part(rows, jnp.bfloat16),
            whole,
            whole,
        ]
        + [pltpu.SemaphoreType.DMA((chunks,))] * 6,
        compiler_params=pltpu.CompilerParams(
            collective_id=9, has_side_effects=True, vmem_limit_bytes=48 * 1024 * 1024
        ),
        name="chain",
    )(coeff, low, high, end, forcing)


def per_device(
    trajectory,
    diffusivity,
    adjoint_end,
    obs_jac,
    obs_value,
    obs_weight,
    obs_valid,
    obs_owner,
    obs_tile,
):
    _, lat_dev, levels, nlon = trajectory.shape
    lats = lax.axis_size("lat")
    devices = lax.axis_size("tm") * lats
    blocks = obs_owner.shape[0]
    slots = max(2, 2 * blocks // devices)
    upward = [(i, i + 1) for i in range(lats - 1)]
    downward = [(i + 1, i) for i in range(lats - 1)]
    low = lax.ppermute(diffusivity[0, lat_dev - SUB :].astype(jnp.bfloat16), "lat", upward)
    high = lax.ppermute(diffusivity[0, :SUB].astype(jnp.bfloat16), "lat", downward)

    ids, slot = route(obs_owner[:, 0], obs_tile, devices, slots)
    wanted = exchange(ids[:, None, :], 1)[:, 0]
    found = gather(wanted, trajectory, slots)
    returned = exchange(found, 2)
    terms = block_terms(
        slot, returned.reshape(devices * PAD, -1), obs_jac, obs_value, obs_weight, obs_valid
    )
    received = exchange(terms.reshape(found.shape), 3)
    forcing = scatter(wanted, received, (lat_dev, levels, nlon), slots)
    return chain(diffusivity, low, high, adjoint_end, forcing)


def solution(mesh):
    in_specs = (
        P("tm", "lat", None, None),
        P("tm", "lat", None, None),
        P("lat", None, None),
        P(("tm", "lat"), None, None),
        P(("tm", "lat"), None),
        P(("tm", "lat"), None),
        P(("tm", "lat"), None),
        P(("tm", "lat"), None),
        P(("tm", "lat")),
    )
    out_specs = P("tm", "lat", None, None)
    return jax.shard_map(
        per_device, mesh=mesh, in_specs=in_specs, out_specs=out_specs, check_vma=False
    )
```

time: 391 us -> 134 us (0.34)
  the two profiles are of different devices: /device:TPU:28 before, /device:TPU:8 now
where the time goes in v1:
time: 134 us; the launch traced here: 133 us
  Pallas kernels  124 us (93%)
  starting transfers between devices  5.84 us (4%)
  other arithmetic  1.73 us (1%)
  local copies, waits for them, and re-layouts  1.43 us (1%)
    pallas_call x1, Pallas kernels, chain(): pl.pallas_call(functools.partial(chain_kernel, lax.axis_size('tm'), lax.a...  54 us
    pallas_call x3, Pallas kernels, exchange(): pl.pallas_call(functools.partial(exchange_kernel, count, lat), out_shape=...  42 us
    pallas_call x1, Pallas kernels, scatter(): pl.pallas_call(functools.partial(scatter_kernel, slots), out_shape=jax.Sh...  8.76 us
    pallas_call x1, Pallas kernels, gather(): pl.pallas_call(functools.partial(gather_kernel, slots), out_shape=jax.Sha...  8.67 us
    pallas_call x1, Pallas kernels, block_terms(): pl.pallas_call(blocks_kernel, out_shape=jax.ShapeDtypeStruct(states.shape...  7.77 us
    ppermute x1, starting transfers between devices, per_device(): lax.ppermute(diffusivity[0, :SUB].astype(jnp.bfloat16), 'lat', downward)  3.29 us
  transfers between devices with their start and end apart: 2, of which 0 were waited for; matrix products, arithmetic and copies ran while one was open for 0% of the time, Pallas kernels for 53%

profile of v1, /device:TPU:8, one launch (start us, length us, event | category | flops | bytes accessed | tf_op | source)
XLA Modules:
  0.0 133.0 jit_solution(17056844340768544031)
XLA Ops:
  0.0 1.7 %convert.4 = bf16[1,4,64,2048]{3,2,1,0:T(8,128)(2,1)S(1)} convert(f32[1,4,64,2048]{3,2,1,0:T(8,128)} %coeff_ref.1) | non-fusion elementwise | flops 524288 | bytes 3145728 | tf_op jit(solution)/shard_map/convert.1
  1.7 0.1 slice_bitcast_fusion
  1.8 3.3 %collective-permute-start.1 = (bf16[2,64,2048]{2,1,0:T(8,128)(2,1)S(1)}, bf16[2,64,2048]{2,1,0:T(8,128)(2,1)S(1)}, u32[]{:S(2)}, u32[]{:S(2)}) collective-permute-start(bf16[2,64,2048]{2,1,0:T(8,128)(2,1)S(1)} %get-tuple-element.9), channel_id=1, source_target_pairs={{1,0},{2,1},{3,2},{4,3},{5,4},{6,5},{7,6},{9,8},{10,9},{11,10},{12... | collective-permute-start | bytes 1572872 | tf_op jit(solution)/shard_map/ppermute | solution.py:437
  5.1 2.6 %collective-permute-start = (bf16[2,64,2048]{2,1,0:T(8,128)(2,1)S(1)}, bf16[2,64,2048]{2,1,0:T(8,128)(2,1)S(1)}, u32[]{:S(2)}, u32[]{:S(2)}) collective-permute-start(bf16[2,64,2048]{2,1,0:T(8,128)(2,1)S(1)} %get-tuple-element.10), channel_id=1, source_target_pairs={{0,1},{1,2},{2,3},{3,4},{4,5},{5,6},{6,7},{8,9},{9,10},{10,11},{11... | collective-permute-start | bytes 1572872 | tf_op jit(solution)/shard_map/ppermute | solution.py:436
  7.7 2.7 %route.1 = (s32[32,128]{1,0:T(8,128)}, s32[96]{0:T(128)}) custom-call(s32[96]{0:T(128)} %bitcast.14, s32[96]{0:T(128)} %tile_ref.1), custom_call_target="tpu_custom_call" | custom-call | tf_op jit(solution)/shard_map/route/pallas_call | solution.py:43
  10.4 20.7 %exchange1.1 = s32[32,1,128]{2,1,0:T(1,128)} custom-call(s32[32,1,128]{2,1,0:T(1,128)} %bitcast.13), custom_call_target="tpu_custom_call" | custom-call | tf_op jit(solution)/shard_map/exchange1/pallas_call | solution.py:109
  31.0 8.7 %gather.1.x_ref = f32[32,8,128]{2,1,0:T(8,128)} custom-call(s32[32,128]{1,0:T(8,128)} %bitcast.11, f32[1,4,64,2048]{3,2,1,0:T(8,128)} %traj_ref.1), custom_call_target="tpu_custom_call" | custom-call | tf_op jit(solution)/shard_map/gather/pallas_call | solution.py:157
  39.7 10.7 %exchange2.1 = f32[32,8,128]{2,1,0:T(8,128)} custom-call(f32[32,8,128]{2,1,0:T(8,128)} %gather.1.x_ref), custom_call_target="tpu_custom_call" | custom-call | tf_op jit(solution)/shard_map/exchange2/pallas_call | solution.py:109
  50.4 7.8 %blocks.1 = f32[256,128]{1,0:T(8,128)} custom-call(s32[96]{0:T(128)} %get-tuple-element.8.slot_ref, f32[256,128]{1,0:T(8,128)} %bitcast.9, bf16[96,128,128]{2,1,0:T(8,128)(2,1)} %jac_ref.1, f32[96,128]{1,0:T(8,128)} %value_ref.1, f32[96,128]{1,0:T(8,128)} %weight_ref.1, s32[96,128]{1,0:T(8,128)} %valid_ref.1), custom_call_target="tpu_custom_call" | custom-call | tf_op jit(solution)/shard_map/blocks/pallas_call | solution.py:202
  58.2 0.0 copy-start
  58.2 10.7 %exchange3.1.terms_ref = f32[32,8,128]{2,1,0:T(8,128)} custom-call(f32[32,8,128]{2,1,0:T(8,128)} %bitcast.10), custom_call_target="tpu_custom_call" | custom-call | tf_op jit(solution)/shard_map/exchange3/pallas_call | solution.py:109
  68.9 8.8 %scatter.1.forcing_ref = f32[4,64,2048]{2,1,0:T(8,128)} custom-call(s32[32,128]{1,0:T(8,128)} %bitcast.12, f32[32,8,128]{2,1,0:T(8,128)} %exchange3.1.terms_ref), custom_call_target="tpu_custom_call" | custom-call | tf_op jit(solution)/shard_map/scatter/pallas_call | solution.py:233
  77.6 0.0 collective-permute-done.1.high_ref
  77.6 0.0 collective-permute-done.low_ref
  77.6 0.0 copy-done
  77.7 54.0 %chain.1 = f32[1,4,64,2048]{3,2,1,0:T(8,128)S(1)} custom-call(f32[1,4,64,2048]{3,2,1,0:T(8,128)} %coeff_ref.1, bf16[2,64,2048]{2,1,0:T(8,128)(2,1)S(1)} %collective-permute-done.low_ref, bf16[2,64,2048]{2,1,0:T(8,128)(2,1)S(1)} %collective-permute-done.1.high_ref, bf16[4,64,2048]{2,1,0:T(8,128)(2,1)S(1)} %copy-done, f32[4,64,2048]{2,1,0:T(8,128)} %scatter.1.forcing_ref), custom_call_target="tpu_custom_call" | custom-call | tf_op jit(solution)/shard_map/chain/pallas_call | solution.py:397
  131.7 1.3 copy.11
Async XLA Ops:
  1.8 75.8 %collective-permute-start.1 = (bf16[2,64,2048]{2,1,0:T(8,128)(2,1)S(1)}, bf16[2,64,2048]{2,1,0:T(8,128)(2,1)S(1)}, u32[]{:S(2)}, u32[]{:S(2)}) collective-permute-start(bf16[2,64,2048]{2,1,0:T(8,128)(2,1)S(1)} %get-tuple-element.9), channel_id=1, source_target_pairs={{1,0},{2,1},{3,2},{4,3},{5,4},{6,5},{7,6},{9,8},{10,9},{11,10},{12... | collective-permute-start | bytes 1572872 | tf_op jit(solution)/shard_map/ppermute | solution.py:437
  5.1 72.5 %collective-permute-start = (bf16[2,64,2048]{2,1,0:T(8,128)(2,1)S(1)}, bf16[2,64,2048]{2,1,0:T(8,128)(2,1)S(1)}, u32[]{:S(2)}, u32[]{:S(2)}) collective-permute-start(bf16[2,64,2048]{2,1,0:T(8,128)(2,1)S(1)} %get-tuple-element.10), channel_id=1, source_target_pairs={{0,1},{1,2},{2,3},{3,4},{4,5},{5,6},{6,7},{8,9},{9,10},{10,11},{11... | collective-permute-start | bytes 1572872 | tf_op jit(solution)/shard_map/ppermute | solution.py:436
  58.2 19.5 %copy-start = (bf16[4,64,2048]{2,1,0:T(8,128)(2,1)S(1)}, bf16[4,64,2048]{2,1,0:T(8,128)(2,1)}, u32[]{:S(2)}) copy-start(bf16[4,64,2048]{2,1,0:T(8,128)(2,1)} %end_ref.1) | copy-start | bytes 3145732

commit v2 on v1

--- a/solution.py
+++ b/solution.py
@@ -241,7 +241,7 @@
 
 def chain_kernel(
     sections, lats, coeff_ref, low_ref, high_ref, end_ref, forcing_ref, out_ref,
-    main, low, high, ahead, first_buf, second_buf,
+    main, low, high, edge_low, edge_high, ahead, weighted, partial, second,
     main_send, main_recv, down_send, up_send, low_recv, high_recv,
 ):
     section, band = lax.axis_index("tm"), lax.axis_index("lat")
@@ -277,10 +277,10 @@
         return remote(ahead.at[c], main.at[c], main_send.at[c], main_recv.at[c], section - 1, band)
 
     def downward(c):
-        return remote(main.at[c, pl.ds(0, SUB)], high.at[c], down_send.at[c], high_recv.at[c], section, band - 1)
+        return remote(edge_low.at[c], high.at[c], down_send.at[c], high_recv.at[c], section, band - 1)
 
     def upward(c):
-        return remote(main.at[c, pl.ds(rows - SUB, SUB)], low.at[c], up_send.at[c], low_recv.at[c], section, band + 1)
+        return remote(edge_high.at[c], low.at[c], up_send.at[c], low_recv.at[c], section, band + 1)
 
     @pl.when(jnp.logical_not(has_low))
     def _():
@@ -295,7 +295,13 @@
         for c in range(chunks):
             local_main(c).start()
 
-    def pass_edges(c):
+    def levels_of(c):
+        return pl.ds(pl.multiple_of(c * CHUNK, CHUNK), CHUNK)
+
+    def along(mid):
+        return pltpu.roll(mid, 1, 1) + pltpu.roll(mid, nlon - 1, 1) - 4.0 * mid
+
+    def begin(c):
         @pl.when(is_last)
         def _():
             local_main(c).wait()
@@ -304,6 +310,24 @@
         def _():
             handed(c).wait_recv()
 
+        span = levels_of(c)
+        for r in range(rows):
+            weighted[c, r] = coeff_ref[0, r, span, :] * main[c, r].astype(jnp.float32)
+        for r in range(rows):
+            mid = weighted[c, r]
+            value = main[c, r].astype(jnp.float32) + along(mid)
+            if r > 0:
+                value = value + weighted[c, r - 1]
+            if r < rows - 1:
+                value = value + weighted[c, r + 1]
+            partial[c, r] = value
+            if r == 0:
+                edge_low[c, 0] = mid.astype(jnp.bfloat16)
+                edge_low[c, 1] = (coeff_ref[0, r, span, :] * value).astype(jnp.bfloat16)
+            if r == rows - 1:
+                edge_high[c, 0] = mid.astype(jnp.bfloat16)
+                edge_high[c, 1] = (coeff_ref[0, r, span, :] * value).astype(jnp.bfloat16)
+
         @pl.when(has_low)
         def _():
             downward(c).start()
@@ -312,46 +336,26 @@
         def _():
             upward(c).start()
 
-    def compute(c):
-        span = pl.ds(pl.multiple_of(c * CHUNK, CHUNK), CHUNK)
-        total = rows + 2 * SUB
-
-        def field(i):
-            if i < SUB:
-                return low[c, i].astype(jnp.float32)
-            if i < SUB + rows:
-                return main[c, i - SUB].astype(jnp.float32)
-            return high[c, i - SUB - rows].astype(jnp.float32)
-
-        def coeff(i):
-            if i < SUB:
-                return low_ref[i, span, :].astype(jnp.float32)
-            if i < SUB + rows:
-                return coeff_ref[0, i - SUB, span, :]
-            return high_ref[i - SUB - rows, span, :].astype(jnp.float32)
-
-        def spread(buf, i):
-            mid = buf[i]
-            return buf[i + 1] + buf[i - 1] + pltpu.roll(mid, 1, 1) + pltpu.roll(mid, nlon - 1, 1) - 4.0 * mid
-
-        for i in range(total):
-            first_buf[i] = coeff(i) * field(i)
-        for i in range(1, total - 1):
-            value = field(i) + spread(first_buf, i)
-            second_buf[i] = coeff(i) * value
-            if SUB <= i < SUB + rows:
-                out_ref[0, i - SUB, span, :] = forcing_ref[i - SUB, span, :] + value
+    def complete(c):
+        span = levels_of(c)
+        end = rows - 1
+        partial[c, 0] = partial[c, 0] + low[c, 0].astype(jnp.float32)
+        partial[c, end] = partial[c, end] + high[c, 0].astype(jnp.float32)
+        second[0] = low[c, 1].astype(jnp.float32) + low_ref[0, span, :].astype(jnp.float32) * weighted[c, 0]
+        second[rows + 1] = high[c, 1].astype(jnp.float32) + high_ref[0, span, :].astype(jnp.float32) * weighted[c, end]
         for r in range(rows):
-            value = out_ref[0, r, span, :] + spread(second_buf, r + SUB)
+            second[r + 1] = coeff_ref[0, r, span, :] * partial[c, r]
+        for r in range(rows):
+            value = partial[c, r] + second[r] + second[r + 2] + along(second[r + 1]) + forcing_ref[r, span, :]
             out_ref[0, r, span, :] = value
             ahead[c, r] = value.astype(jnp.bfloat16)
 
-    pass_edges(0)
+    begin(0)
 
     def step(c, carry):
         @pl.when(c + 1 < chunks)
         def _():
-            pass_edges(c + 1)
+            begin(c + 1)
 
         @pl.when(has_low)
         def _():
@@ -361,7 +365,7 @@
         def _():
             downward(c).wait_recv()
 
-        compute(c)
+        complete(c)
 
         @pl.when(has_before)
         def _():
@@ -393,7 +397,6 @@
     rows, levels, nlon = end.shape
     chunks = levels // CHUNK
     part = lambda n, kind: pltpu.VMEM((chunks, n, CHUNK, nlon), kind)
-    whole = pltpu.VMEM((rows + 2 * SUB, CHUNK, nlon), jnp.float32)
     return pl.pallas_call(
         functools.partial(chain_kernel, lax.axis_size("tm"), lax.axis_size("lat")),
         out_shape=jax.ShapeDtypeStruct(coeff.shape, jnp.float32),
@@ -403,9 +406,12 @@
             part(rows, jnp.bfloat16),
             part(SUB, jnp.bfloat16),
             part(SUB, jnp.bfloat16),
+            part(SUB, jnp.bfloat16),
+            part(SUB, jnp.bfloat16),
             part(rows, jnp.bfloat16),
-            whole,
-            whole,
+            part(rows, jnp.float32),
+            part(rows, jnp.float32),
+            pltpu.VMEM((rows + 2, CHUNK, nlon), jnp.float32),
         ]
         + [pltpu.SemaphoreType.DMA((chunks,))] * 6,
         compiler_params=pltpu.CompilerParams(
@@ -433,11 +439,12 @@
     slots = max(2, 2 * blocks // devices)
     upward = [(i, i + 1) for i in range(lats - 1)]
     downward = [(i + 1, i) for i in range(lats - 1)]
-    low = lax.ppermute(diffusivity[0, lat_dev - SUB :].astype(jnp.bfloat16), "lat", upward)
-    high = lax.ppermute(diffusivity[0, :SUB].astype(jnp.bfloat16), "lat", downward)
-
     ids, slot = route(obs_owner[:, 0], obs_tile, devices, slots)
     wanted = exchange(ids[:, None, :], 1)[:, 0]
+    edges = lax.optimization_barrier((diffusivity[0, :1], diffusivity[0, lat_dev - 1 :], wanted))
+    wanted = edges[2]
+    low = lax.ppermute(edges[1].astype(jnp.bfloat16), "lat", upward)
+    high = lax.ppermute(edges[0].astype(jnp.bfloat16), "lat", downward)
     found = gather(wanted, trajectory, slots)
     returned = exchange(found, 2)
     terms = block_terms(

time: 134 us -> 124 us (0.925)
  Pallas kernels: 124 us -> 112 us
  local copies, waits for them, and re-layouts: 1.43 us -> 3.39 us
  other arithmetic: 1.73 us -> 0 us
    pallas_call x3, Pallas kernels: 42 us -> 31 us  [exchange(): pl.pallas_call(functools.partial(exchange_kernel, count, lat), out_shape=...]
    squeeze x0 -> x1, local copies, waits for them, and re-layouts: none -> 2.06 us  [per_device(): diffusivity[0, lat_dev - 1:]]
    another operation x1 -> x0, other arithmetic: 1.73 us -> none
  transfers between devices with their start and end apart: 2 -> 2, of which waited for: 0 -> 0; matrix products, arithmetic and copies ran while one was open for 0% -> 0% of each run, Pallas kernels for 53% -> 38%
where the time goes in v2:
time: 124 us; the launch traced here: 122 us
  Pallas kernels  112 us (90%)
  starting transfers between devices  6.73 us (5%)
  local copies, waits for them, and re-layouts  3.39 us (3%)
    pallas_call x1, Pallas kernels, chain(): pl.pallas_call(functools.partial(chain_kernel, lax.axis_size('tm'), lax.a...  52.9 us
    pallas_call x3, Pallas kernels, exchange(): pl.pallas_call(functools.partial(exchange_kernel, count, lat), out_shape=...  31 us
    pallas_call x1, Pallas kernels, scatter(): pl.pallas_call(functools.partial(scatter_kernel, slots), out_shape=jax.Sh...  8.76 us
    pallas_call x1, Pallas kernels, gather(): pl.pallas_call(functools.partial(gather_kernel, slots), out_shape=jax.Sha...  8.67 us
    pallas_call x1, Pallas kernels, block_terms(): pl.pallas_call(blocks_kernel, out_shape=jax.ShapeDtypeStruct(states.shape...  7.86 us
    ppermute x1, starting transfers between devices, per_device(): high = lax.ppermute(edges[0].astype(jnp.bfloat16), 'lat', downward)  3.4 us
    ppermute x1, starting transfers between devices, per_device(): low = lax.ppermute(edges[1].astype(jnp.bfloat16), 'lat', upward)  3.33 us
    pallas_call x1, Pallas kernels, route(): pl.pallas_call(functools.partial(route_kernel, slots), out_shape=(jax.Sha...  2.67 us
  transfers between devices with their start and end apart: 2, of which 0 were waited for; matrix products, arithmetic and copies ran while one was open for 0% of the time, Pallas kernels for 38%

profile of v2, /device:TPU:8, one launch (start us, length us, event | category | flops | bytes accessed | tf_op | source)
XLA Modules:
  0.0 122.1 jit_solution(1703179240675813157)
XLA Ops:
  0.0 2.7 %route.1 = (s32[32,128]{1,0:T(8,128)}, s32[96]{0:T(128)}) custom-call(s32[96]{0:T(128)} %bitcast.14, s32[96]{0:T(128)} %tile_ref.1), custom_call_target="tpu_custom_call" | custom-call | tf_op jit(solution)/shard_map/route/pallas_call | solution.py:43
  2.7 9.7 %exchange1.1 = s32[32,1,128]{2,1,0:T(1,128)} custom-call(s32[32,1,128]{2,1,0:T(1,128)} %bitcast.13), custom_call_target="tpu_custom_call" | custom-call | tf_op jit(solution)/shard_map/exchange1/pallas_call | solution.py:109
  12.4 2.1 %slice_bitcast_fusion = (bf16[1,64,2048]{2,1,0:T(8,128)(2,1)}, bf16[1,64,2048]{2,1,0:T(8,128)(2,1)}) fusion(f32[1,4,64,2048]{3,2,1,0:T(8,128)} %coeff_ref.1), kind=kLoop, calls=%fused_computation | loop fusion | bytes 1048576 | tf_op jit(solution)/shard_map/squeeze | solution.py:444
  14.5 3.3 %collective-permute-start = (bf16[1,64,2048]{2,1,0:T(8,128)(2,1)}, bf16[1,64,2048]{2,1,0:T(8,128)(2,1)S(1)}, u32[]{:S(2)}, u32[]{:S(2)}) collective-permute-start(bf16[1,64,2048]{2,1,0:T(8,128)(2,1)} %get-tuple-element.11), channel_id=1, source_target_pairs={{0,1},{1,2},{2,3},{3,4},{4,5},{5,6},{6,7},{8,9},{9,10},{10,11},{11... | collective-permute-start | bytes 786440 | tf_op jit(solution)/shard_map/ppermute | solution.py:446
  17.8 3.4 %collective-permute-start.1 = (bf16[1,64,2048]{2,1,0:T(8,128)(2,1)}, bf16[1,64,2048]{2,1,0:T(8,128)(2,1)}, u32[]{:S(2)}, u32[]{:S(2)}) collective-permute-start(bf16[1,64,2048]{2,1,0:T(8,128)(2,1)} %get-tuple-element.12), channel_id=1, source_target_pairs={{1,0},{2,1},{3,2},{4,3},{5,4},{6,5},{7,6},{9,8},{10,9},{11,10},{12... | collective-permute-start | bytes 786440 | tf_op jit(solution)/shard_map/ppermute | solution.py:447
  21.2 8.7 %gather.1.x_ref = f32[32,8,128]{2,1,0:T(8,128)} custom-call(s32[32,128]{1,0:T(8,128)} %bitcast.11, f32[1,4,64,2048]{3,2,1,0:T(8,128)} %traj_ref.1), custom_call_target="tpu_custom_call" | custom-call | tf_op jit(solution)/shard_map/gather/pallas_call | solution.py:157
  29.9 10.5 %exchange2.1 = f32[32,8,128]{2,1,0:T(8,128)} custom-call(f32[32,8,128]{2,1,0:T(8,128)} %gather.1.x_ref), custom_call_target="tpu_custom_call" | custom-call | tf_op jit(solution)/shard_map/exchange2/pallas_call | solution.py:109
  40.4 0.0 copy-start.1
  40.4 7.9 %blocks.1 = f32[256,128]{1,0:T(8,128)} custom-call(s32[96]{0:T(128)} %get-tuple-element.14.slot_ref, f32[256,128]{1,0:T(8,128)} %bitcast.9, bf16[96,128,128]{2,1,0:T(8,128)(2,1)} %jac_ref.1, f32[96,128]{1,0:T(8,128)} %value_ref.1, f32[96,128]{1,0:T(8,128)} %weight_ref.1, s32[96,128]{1,0:T(8,128)} %valid_ref.1), custom_call_target="tpu_custom_call" | custom-call | tf_op jit(solution)/shard_map/blocks/pallas_call | solution.py:202
  48.3 0.0 copy-start
  48.3 10.8 %exchange3.1.terms_ref = f32[32,8,128]{2,1,0:T(8,128)} custom-call(f32[32,8,128]{2,1,0:T(8,128)} %bitcast.10), custom_call_target="tpu_custom_call" | custom-call | tf_op jit(solution)/shard_map/exchange3/pallas_call | solution.py:109
  59.1 8.8 %scatter.1.forcing_ref = f32[4,64,2048]{2,1,0:T(8,128)} custom-call(s32[32,128]{1,0:T(8,128)} %bitcast.12, f32[32,8,128]{2,1,0:T(8,128)} %exchange3.1.terms_ref), custom_call_target="tpu_custom_call" | custom-call | tf_op jit(solution)/shard_map/scatter/pallas_call | solution.py:233
  67.8 0.0 collective-permute-done.low_ref
  67.8 0.0 collective-permute-done.1.high_ref
  67.9 0.0 copy-done.1
  67.9 0.0 copy-done
  67.9 52.9 %chain.1 = f32[1,4,64,2048]{3,2,1,0:T(8,128)S(1)} custom-call(f32[1,4,64,2048]{3,2,1,0:T(8,128)S(1)} %copy-done, bf16[1,64,2048]{2,1,0:T(8,128)(2,1)S(1)} %collective-permute-done.low_ref, bf16[1,64,2048]{2,1,0:T(8,128)(2,1)} %collective-permute-done.1.high_ref, bf16[4,64,2048]{2,1,0:T(8,128)(2,1)S(1)} %copy-done.1, f32[4,64,2048]{2,1,0:T(8,128)} %scatter.1.forcing_ref), custom_call_target="tpu_custom_call" | custom-call | tf_op jit(solution)/shard_map/chain/pallas_call | solution.py:400
  120.8 1.3 %copy.11 = f32[1,4,64,2048]{3,2,1,0:T(8,128)} copy(f32[1,4,64,2048]{3,2,1,0:T(8,128)S(1)} %chain.1) | data formatting | bytes 4194304
Async XLA Ops:
  14.5 53.4 %collective-permute-start = (bf16[1,64,2048]{2,1,0:T(8,128)(2,1)}, bf16[1,64,2048]{2,1,0:T(8,128)(2,1)S(1)}, u32[]{:S(2)}, u32[]{:S(2)}) collective-permute-start(bf16[1,64,2048]{2,1,0:T(8,128)(2,1)} %get-tuple-element.11), channel_id=1, source_target_pairs={{0,1},{1,2},{2,3},{3,4},{4,5},{5,6},{6,7},{8,9},{9,10},{10,11},{11... | collective-permute-start | bytes 786440 | tf_op jit(solution)/shard_map/ppermute | solution.py:446
  17.8 50.0 %collective-permute-start.1 = (bf16[1,64,2048]{2,1,0:T(8,128)(2,1)}, bf16[1,64,2048]{2,1,0:T(8,128)(2,1)}, u32[]{:S(2)}, u32[]{:S(2)}) collective-permute-start(bf16[1,64,2048]{2,1,0:T(8,128)(2,1)} %get-tuple-element.12), channel_id=1, source_target_pairs={{1,0},{2,1},{3,2},{4,3},{5,4},{6,5},{7,6},{9,8},{10,9},{11,10},{12... | collective-permute-start | bytes 786440 | tf_op jit(solution)/shard_map/ppermute | solution.py:447
  40.4 27.4 %copy-start.1 = (bf16[4,64,2048]{2,1,0:T(8,128)(2,1)S(1)}, bf16[4,64,2048]{2,1,0:T(8,128)(2,1)}, u32[]{:S(2)}) copy-start(bf16[4,64,2048]{2,1,0:T(8,128)(2,1)} %end_ref.1) | copy-start | bytes 3145732
  48.3 19.6 %copy-start = (f32[1,4,64,2048]{3,2,1,0:T(8,128)S(1)}, f32[1,4,64,2048]{3,2,1,0:T(8,128)}, u32[]{:S(2)}) copy-start(f32[1,4,64,2048]{3,2,1,0:T(8,128)} %coeff_ref.1) | copy-start | bytes 6291460

commit v3 on v2

--- a/solution.py
+++ b/solution.py
@@ -11,7 +11,7 @@
 SUB = 2
 LANES = 128
 PAD = 8
-CHUNK = 16
+CHUNK = 8
 MESH = pl.DeviceIdType.MESH
 VMEM = pl.BlockSpec(memory_space=pltpu.VMEM)
 SMEM = pl.BlockSpec(memory_space=pltpu.SMEM)
@@ -53,7 +53,11 @@
     )(owner, tile)
 
 
-def exchange_kernel(count, lat, x_ref, out_ref, send_sem, recv_sem, own_sem):
+def exchange_kernel(count, lat, shift, *refs):
+    if shift:
+        x_ref, edge_ref, out_ref, beside_ref, send_sem, recv_sem, own_sem, edge_send, edge_recv = refs
+    else:
+        x_ref, out_ref, send_sem, recv_sem, own_sem = refs
     me = lax.axis_index("tm") * lat + lax.axis_index("lat")
     barrier = pltpu.get_barrier_semaphore()
 
@@ -99,15 +103,88 @@
         return carry
 
     lax.fori_loop(1, count, launch, 0)
+    if shift:
+        band, section = lax.axis_index("lat"), lax.axis_index("tm")
+        is_last = section == count // lat - 1
+        gives = is_last & (band < lat - 1 if shift > 0 else band > 0)
+        takes = is_last & (band > 0 if shift > 0 else band < lat - 1)
+
+        def edge():
+            return pltpu.make_async_remote_copy(
+                src_ref=edge_ref,
+                dst_ref=beside_ref,
+                send_sem=edge_send,
+                recv_sem=edge_recv,
+                device_id=(section, band + shift),
+                device_id_type=MESH,
+            )
+
+        @pl.when(gives)
+        def _():
+            edge().start()
+
+        @pl.when(jnp.logical_not(takes))
+        def _():
+            beside_ref[...] = jnp.zeros_like(beside_ref)
+
     own.wait()
     lax.fori_loop(1, count, land, 0)
-
-
-def exchange(x, collective_id):
+    if shift:
+        @pl.when(takes)
+        def _():
+            edge().wait_recv()
+
+        @pl.when(gives)
+        def _():
+            edge().wait_send()
+
+
+def last_edges_kernel(coeff_ref, end_ref, low_ref, high_ref):
+    rows, levels, nlon = end_ref.shape
+
+    def one(c, carry):
+        span = pl.ds(pl.multiple_of(c * 16, 16), 16)
+
+        def weigh(r):
+            return coeff_ref[0, r, span, :] * end_ref[r, span, :].astype(jnp.float32)
+
+        for r, inner, ref in ((0, 1, low_ref), (rows - 1, rows - 2, high_ref)):
+            mid = weigh(r)
+            value = end_ref[r, span, :].astype(jnp.float32) + weigh(inner)
+            value = value + pltpu.roll(mid, 1, 1) + pltpu.roll(mid, nlon - 1, 1) - 4.0 * mid
+            ref[0, span, :] = mid.astype(jnp.bfloat16)
+            ref[1, span, :] = (coeff_ref[0, r, span, :] * value).astype(jnp.bfloat16)
+        return carry
+
+    lax.fori_loop(0, levels // 16, one, 0)
+
+
+def last_edges(coeff, end):
+    edge = jax.ShapeDtypeStruct((2,) + end.shape[1:], jnp.bfloat16)
+    return pl.pallas_call(
+        last_edges_kernel,
+        out_shape=(edge, edge),
+        in_specs=[VMEM, VMEM],
+        out_specs=(VMEM, VMEM),
+        name="last_edges",
+    )(coeff, end)
+
+
+def exchange(x, collective_id, edge=None, shift=0):
     lat = lax.axis_size("lat")
     count = lax.axis_size("tm") * lat
-    return pl.pallas_call(
-        functools.partial(exchange_kernel, count, lat),
+    if shift:
+        return pl.pallas_call(
+            functools.partial(exchange_kernel, count, lat, shift),
+            out_shape=(jax.ShapeDtypeStruct(x.shape, x.dtype), jax.ShapeDtypeStruct(edge.shape, edge.dtype)),
+            in_specs=[VMEM, VMEM],
+            out_specs=(VMEM, VMEM),
+            scratch_shapes=[pltpu.SemaphoreType.DMA((count,))] * 2 + [pltpu.SemaphoreType.DMA] * 3,
+            compiler_params=pltpu.CompilerParams(collective_id=collective_id, has_side_effects=True),
+            name="exchange%d" % collective_id,
+        )(x, edge)
+    return pl.pallas_call(
+        functools.partial(exchange_kernel, count, lat, 0),
         out_shape=jax.ShapeDtypeStruct(x.shape, x.dtype),
         in_specs=[VMEM],
         out_specs=VMEM,
@@ -240,7 +317,7 @@
 
 
 def chain_kernel(
-    sections, lats, coeff_ref, low_ref, high_ref, end_ref, forcing_ref, out_ref,
+    sections, lats, coeff_ref, low_ref, high_ref, last_low_ref, last_high_ref, end_ref, forcing_ref, out_ref,
     main, low, high, edge_low, edge_high, ahead, weighted, partial, second,
     main_send, main_recv, down_send, up_send, low_recv, high_recv,
 ):
@@ -249,6 +326,8 @@
     chunks = levels // CHUNK
     is_last = section == sections - 1
     has_before, has_low, has_high = section > 0, band > 0, band < lats - 1
+
+    sends_low, sends_high = has_low & jnp.logical_not(is_last), has_high & jnp.logical_not(is_last)
 
     barrier = pltpu.get_barrier_semaphore()
     sides = (
@@ -294,6 +373,8 @@
     def _():
         for c in range(chunks):
             local_main(c).start()
+            low[c] = last_low_ref[:, c * CHUNK : (c + 1) * CHUNK, :]
+            high[c] = last_high_ref[:, c * CHUNK : (c + 1) * CHUNK, :]
 
     def levels_of(c):
         return pl.ds(pl.multiple_of(c * CHUNK, CHUNK), CHUNK)
@@ -328,11 +409,11 @@
                 edge_high[c, 0] = mid.astype(jnp.bfloat16)
                 edge_high[c, 1] = (coeff_ref[0, r, span, :] * value).astype(jnp.bfloat16)
 
-        @pl.when(has_low)
+        @pl.when(sends_low)
         def _():
             downward(c).start()
 
-        @pl.when(has_high)
+        @pl.when(sends_high)
         def _():
             upward(c).start()
 
@@ -357,11 +438,11 @@
         def _():
             begin(c + 1)
 
-        @pl.when(has_low)
+        @pl.when(sends_low)
         def _():
             upward(c).wait_recv()
 
-        @pl.when(has_high)
+        @pl.when(sends_high)
         def _():
             downward(c).wait_recv()
 
@@ -376,11 +457,11 @@
     lax.fori_loop(0, chunks, step, 0)
 
     def finish(c, carry):
-        @pl.when(has_low)
+        @pl.when(sends_low)
         def _():
             downward(c).wait_send()
 
-        @pl.when(has_high)
+        @pl.when(sends_high)
         def _():
             upward(c).wait_send()
 
@@ -393,14 +474,14 @@
     lax.fori_loop(0, chunks, finish, 0)
 
 
-def chain(coeff, low, high, end, forcing):
+def chain(coeff, low, high, last_low, last_high, end, forcing):
     rows, levels, nlon = end.shape
     chunks = levels // CHUNK
     part = lambda n, kind: pltpu.VMEM((chunks, n, CHUNK, nlon), kind)
     return pl.pallas_call(
         functools.partial(chain_kernel, lax.axis_size("tm"), lax.axis_size("lat")),
         out_shape=jax.ShapeDtypeStruct(coeff.shape, jnp.float32),
-        in_specs=[VMEM] * 5,
+        in_specs=[VMEM] * 7,
         out_specs=VMEM,
         scratch_shapes=[
             part(rows, jnp.bfloat16),
@@ -418,7 +499,7 @@
             collective_id=9, has_side_effects=True, vmem_limit_bytes=48 * 1024 * 1024
         ),
         name="chain",
-    )(coeff, low, high, end, forcing)
+    )(coeff, low, high, last_low, last_high, end, forcing)
 
 
 def per_device(
@@ -446,13 +527,14 @@
     low = lax.ppermute(edges[1].astype(jnp.bfloat16), "lat", upward)
     high = lax.ppermute(edges[0].astype(jnp.bfloat16), "lat", downward)
     found = gather(wanted, trajectory, slots)
-    returned = exchange(found, 2)
+    edge_low, edge_high = last_edges(diffusivity, adjoint_end)
+    returned, last_low = exchange(found, 2, edge_high, 1)
     terms = block_terms(
         slot, returned.reshape(devices * PAD, -1), obs_jac, obs_value, obs_weight, obs_valid
     )
-    received = exchange(terms.reshape(found.shape), 3)
+    received, last_high = exchange(terms.reshape(found.shape), 3, edge_low, -1)
     forcing = scatter(wanted, received, (lat_dev, levels, nlon), slots)
-    return chain(diffusivity, low, high, adjoint_end, forcing)
+    return chain(diffusivity, low, high, last_low, last_high, adjoint_end, forcing)
 
 
 def solution(mesh):

time: 124 us -> 127 us (1.024)
  Pallas kernels: 112 us -> 115 us
    pallas_call x3 -> x4, Pallas kernels: 31 us -> 39.2 us  [the longest x2 25.9 us: exchange(): pl.pallas_call(functools.partial(exchange_kernel, count, lat, shift), out...]
    pallas_call x1, Pallas kernels: 52.9 us -> 48.3 us  [chain(): pl.pallas_call(functools.partial(chain_kernel, lax.axis_size('tm'), lax.a...]
  transfers between devices with their start and end apart: 2 -> 2, of which waited for: 0 -> 0; matrix products, arithmetic and copies ran while one was open for 0% -> 0% of each run, Pallas kernels for 38% -> 44%
where the time goes in v3:
time: 127 us; the launch traced here: 125 us
  Pallas kernels  115 us (91%)
  starting transfers between devices  6.74 us (5%)
  local copies, waits for them, and re-layouts  2.6 us (2%)
    pallas_call x1, Pallas kernels, chain(): pl.pallas_call(functools.partial(chain_kernel, lax.axis_size('tm'), lax.a...  48.3 us
    pallas_call x2, Pallas kernels, exchange(): pl.pallas_call(functools.partial(exchange_kernel, count, lat, shift), out...  25.9 us
    pallas_call x1, Pallas kernels, exchange(): pl.pallas_call(functools.partial(exchange_kernel, count, lat, 0), out_sha...  9.72 us
    pallas_call x1, Pallas kernels, scatter(): pl.pallas_call(functools.partial(scatter_kernel, slots), out_shape=jax.Sh...  8.9 us
    pallas_call x1, Pallas kernels, gather(): pl.pallas_call(functools.partial(gather_kernel, slots), out_shape=jax.Sha...  8.66 us
    pallas_call x1, Pallas kernels, block_terms(): pl.pallas_call(blocks_kernel, out_shape=jax.ShapeDtypeStruct(states.shape...  7.76 us
    pallas_call x1, Pallas kernels, last_edges(): pl.pallas_call(last_edges_kernel, out_shape=(edge, edge), in_specs=[VMEM,...  3.6 us
    ppermute x1, starting transfers between devices, per_device(): high = lax.ppermute(edges[0].astype(jnp.bfloat16), 'lat', downward)  3.4 us
  transfers between devices with their start and end apart: 2, of which 0 were waited for; matrix products, arithmetic and copies ran while one was open for 0% of the time, Pallas kernels for 44%

profile of v3, /device:TPU:8, one launch (start us, length us, event | category | flops | bytes accessed | tf_op | source)
XLA Modules:
  0.0 124.9 jit_solution(12961797198251656528)
XLA Ops:
  0.0 2.7 %route.1 = (s32[32,128]{1,0:T(8,128)}, s32[96]{0:T(128)}) custom-call(s32[96]{0:T(128)} %bitcast.14, s32[96]{0:T(128)} %tile_ref.1), custom_call_target="tpu_custom_call" | custom-call | tf_op jit(solution)/shard_map/route/pallas_call | solution.py:43
  2.7 9.7 %exchange1.1 = s32[32,1,128]{2,1,0:T(1,128)} custom-call(s32[32,1,128]{2,1,0:T(1,128)} %bitcast.13), custom_call_target="tpu_custom_call" | custom-call | tf_op jit(solution)/shard_map/exchange1/pallas_call | solution.py:186
  12.4 1.3 %slice_bitcast_fusion = (bf16[1,64,2048]{2,1,0:T(8,128)(2,1)S(1)}, bf16[1,64,2048]{2,1,0:T(8,128)(2,1)S(1)}) fusion(f32[1,4,64,2048]{3,2,1,0:T(8,128)} %coeff_ref.3), kind=kLoop, calls=%fused_computation | loop fusion | bytes 1048576 | tf_op jit(solution)/shard_map/squeeze | solution.py:525
  13.7 3.3 %collective-permute-start = (bf16[1,64,2048]{2,1,0:T(8,128)(2,1)S(1)}, bf16[1,64,2048]{2,1,0:T(8,128)(2,1)S(1)}, u32[]{:S(2)}, u32[]{:S(2)}) collective-permute-start(bf16[1,64,2048]{2,1,0:T(8,128)(2,1)S(1)} %get-tuple-element.17), channel_id=1, source_target_pairs={{0,1},{1,2},{2,3},{3,4},{4,5},{5,6},{6,7},{8,9},{9,10},{10,11},{11... | collective-permute-start | bytes 786440 | tf_op jit(solution)/shard_map/ppermute | solution.py:527
  17.0 3.4 %collective-permute-start.1 = (bf16[1,64,2048]{2,1,0:T(8,128)(2,1)S(1)}, bf16[1,64,2048]{2,1,0:T(8,128)(2,1)S(1)}, u32[]{:S(2)}, u32[]{:S(2)}) collective-permute-start(bf16[1,64,2048]{2,1,0:T(8,128)(2,1)S(1)} %get-tuple-element.18), channel_id=1, source_target_pairs={{1,0},{2,1},{3,2},{4,3},{5,4},{6,5},{7,6},{9,8},{10,9},{11,10},{12... | collective-permute-start | bytes 786440 | tf_op jit(solution)/shard_map/ppermute | solution.py:528
  20.4 3.6 %last_edges.1 = (bf16[2,64,2048]{2,1,0:T(8,128)(2,1)}, bf16[2,64,2048]{2,1,0:T(8,128)(2,1)}) custom-call(f32[1,4,64,2048]{3,2,1,0:T(8,128)} %coeff_ref.3, bf16[4,64,2048]{2,1,0:T(8,128)(2,1)} %end_ref.3), custom_call_target="tpu_custom_call" | custom-call | tf_op jit(solution)/shard_map/last_edges/pallas_call | solution.py:164
  24.0 8.7 %gather.1.refs_0_ = f32[32,8,128]{2,1,0:T(8,128)} custom-call(s32[32,128]{1,0:T(8,128)} %bitcast.10, f32[1,4,64,2048]{3,2,1,0:T(8,128)} %traj_ref.1), custom_call_target="tpu_custom_call" | custom-call | tf_op jit(solution)/shard_map/gather/pallas_call | solution.py:234
  32.7 11.0 %exchange2.1 = (f32[32,8,128]{2,1,0:T(8,128)}, bf16[2,64,2048]{2,1,0:T(8,128)(2,1)}) custom-call(f32[32,8,128]{2,1,0:T(8,128)} %gather.1.refs_0_, bf16[2,64,2048]{2,1,0:T(8,128)(2,1)} %get-tuple-element.20.refs_1_), custom_call_target="tpu_custom_call" | custom-call | tf_op jit(solution)/shard_map/exchange2/pallas_call | solution.py:177
  43.7 7.8 %blocks.1 = f32[256,128]{1,0:T(8,128)} custom-call(s32[96]{0:T(128)} %get-tuple-element.22.slot_ref, f32[256,128]{1,0:T(8,128)} %bitcast.12, bf16[96,128,128]{2,1,0:T(8,128)(2,1)} %jac_ref.1, f32[96,128]{1,0:T(8,128)} %value_ref.1, f32[96,128]{1,0:T(8,128)} %weight_ref.1, s32[96,128]{1,0:T(8,128)} %valid_ref.1), custom_call_target="tpu_custom_call" | custom-call | tf_op jit(solution)/shard_map/blocks/pallas_call | solution.py:279
  51.5 0.0 copy-start
  51.5 0.0 copy-start.1
  51.5 14.8 %exchange3.1 = (f32[32,8,128]{2,1,0:T(8,128)}, bf16[2,64,2048]{2,1,0:T(8,128)(2,1)}) custom-call(f32[32,8,128]{2,1,0:T(8,128)} %bitcast.9, bf16[2,64,2048]{2,1,0:T(8,128)(2,1)} %get-tuple-element.24.refs_1_), custom_call_target="tpu_custom_call" | custom-call | tf_op jit(solution)/shard_map/exchange3/pallas_call | solution.py:177
  66.3 0.0 copy-start.2
  66.4 8.9 %scatter.1.forcing_ref = f32[4,64,2048]{2,1,0:T(8,128)} custom-call(s32[32,128]{1,0:T(8,128)} %bitcast.11, f32[32,8,128]{2,1,0:T(8,128)} %get-tuple-element.26.terms_ref), custom_call_target="tpu_custom_call" | custom-call | tf_op jit(solution)/shard_map/scatter/pallas_call | solution.py:310
  75.3 0.0 collective-permute-done.low_ref
  75.3 0.0 collective-permute-done.1.high_ref
  75.3 0.0 copy-done
  75.3 0.0 copy-done.1
  75.3 0.0 copy-done.2
  75.3 48.3 %chain.1 = f32[1,4,64,2048]{3,2,1,0:T(8,128)S(1)} custom-call(f32[1,4,64,2048]{3,2,1,0:T(8,128)} %coeff_ref.3, bf16[1,64,2048]{2,1,0:T(8,128)(2,1)S(1)} %collective-permute-done.low_ref, bf16[1,64,2048]{2,1,0:T(8,128)(2,1)S(1)} %collective-permute-done.1.high_ref, bf16[2,64,2048]{2,1,0:T(8,128)(2,1)S(1)} %copy-done.1, bf16[2,64,2048]{2,1,0:T(8,128)(2,1)S(1)} %copy-done.2, ...), custom_call_target="tpu_custom_call" | custom-call | tf_op jit(solution)/shard_map/chain/pallas_call | solution.py:481
  123.6 1.3 %copy.11 = f32[1,4,64,2048]{3,2,1,0:T(8,128)} copy(f32[1,4,64,2048]{3,2,1,0:T(8,128)S(1)} %chain.1) | data formatting | bytes 4194304
Async XLA Ops:
  13.7 61.6 %collective-permute-start = (bf16[1,64,2048]{2,1,0:T(8,128)(2,1)S(1)}, bf16[1,64,2048]{2,1,0:T(8,128)(2,1)S(1)}, u32[]{:S(2)}, u32[]{:S(2)}) collective-permute-start(bf16[1,64,2048]{2,1,0:T(8,128)(2,1)S(1)} %get-tuple-element.17), channel_id=1, source_target_pairs={{0,1},{1,2},{2,3},{3,4},{4,5},{5,6},{6,7},{8,9},{9,10},{10,11},{11... | collective-permute-start | bytes 786440 | tf_op jit(solution)/shard_map/ppermute | solution.py:527
  17.0 58.2 %collective-permute-start.1 = (bf16[1,64,2048]{2,1,0:T(8,128)(2,1)S(1)}, bf16[1,64,2048]{2,1,0:T(8,128)(2,1)S(1)}, u32[]{:S(2)}, u32[]{:S(2)}) collective-permute-start(bf16[1,64,2048]{2,1,0:T(8,128)(2,1)S(1)} %get-tuple-element.18), channel_id=1, source_target_pairs={{1,0},{2,1},{3,2},{4,3},{5,4},{6,5},{7,6},{9,8},{10,9},{11,10},{12... | collective-permute-start | bytes 786440 | tf_op jit(solution)/shard_map/ppermute | solution.py:528
  51.5 23.8 %copy-start = (bf16[4,64,2048]{2,1,0:T(8,128)(2,1)S(1)}, bf16[4,64,2048]{2,1,0:T(8,128)(2,1)}, u32[]{:S(2)}) copy-start(bf16[4,64,2048]{2,1,0:T(8,128)(2,1)} %end_ref.3) | copy-start | bytes 3145732
  51.5 23.8 %copy-start.1 = (bf16[2,64,2048]{2,1,0:T(8,128)(2,1)S(1)}, bf16[2,64,2048]{2,1,0:T(8,128)(2,1)}, u32[]{:S(2)}) copy-start(bf16[2,64,2048]{2,1,0:T(8,128)(2,1)} %get-tuple-element.21.last_low_ref) | copy-start | bytes 1572868
  66.3 8.9 %copy-start.2 = (bf16[2,64,2048]{2,1,0:T(8,128)(2,1)S(1)}, bf16[2,64,2048]{2,1,0:T(8,128)(2,1)}, u32[]{:S(2)}) copy-start(bf16[2,64,2048]{2,1,0:T(8,128)(2,1)} %get-tuple-element.25.last_high_ref) | copy-start | bytes 1572868

commit v4 on v3

--- a/solution.py
+++ b/solution.py
@@ -139,7 +139,7 @@
             edge().wait_send()
 
 
-def last_edges_kernel(coeff_ref, end_ref, low_ref, high_ref):
+def last_edges_kernel(coeff_ref, end_ref, low_ref, high_ref, first_ref, final_ref):
     rows, levels, nlon = end_ref.shape
 
     def one(c, carry):
@@ -154,6 +154,8 @@
             value = value + pltpu.roll(mid, 1, 1) + pltpu.roll(mid, nlon - 1, 1) - 4.0 * mid
             ref[0, span, :] = mid.astype(jnp.bfloat16)
             ref[1, span, :] = (coeff_ref[0, r, span, :] * value).astype(jnp.bfloat16)
+        first_ref[0, span, :] = coeff_ref[0, 0, span, :].astype(jnp.bfloat16)
+        final_ref[0, span, :] = coeff_ref[0, rows - 1, span, :].astype(jnp.bfloat16)
         return carry
 
     lax.fori_loop(0, levels // 16, one, 0)
@@ -161,11 +163,12 @@
 
 def last_edges(coeff, end):
     edge = jax.ShapeDtypeStruct((2,) + end.shape[1:], jnp.bfloat16)
+    single = jax.ShapeDtypeStruct((1,) + end.shape[1:], jnp.bfloat16)
     return pl.pallas_call(
         last_edges_kernel,
-        out_shape=(edge, edge),
+        out_shape=(edge, edge, single, single),
         in_specs=[VMEM, VMEM],
-        out_specs=(VMEM, VMEM),
+        out_specs=(VMEM,) * 4,
         name="last_edges",
     )(coeff, end)
 
@@ -431,12 +434,18 @@
             out_ref[0, r, span, :] = value
             ahead[c, r] = value.astype(jnp.bfloat16)
 
-    begin(0)
+    look = jnp.where(section == sections - 2, min(4, chunks), min(2, chunks))
+
+    def open_one(c, carry):
+        begin(c)
+        return carry
+
+    lax.fori_loop(0, look, open_one, 0)
 
     def step(c, carry):
-        @pl.when(c + 1 < chunks)
-        def _():
-            begin(c + 1)
+        @pl.when(c + look < chunks)
+        def _():
+            begin(c + look)
 
         @pl.when(sends_low)
         def _():
@@ -522,12 +531,12 @@
     downward = [(i + 1, i) for i in range(lats - 1)]
     ids, slot = route(obs_owner[:, 0], obs_tile, devices, slots)
     wanted = exchange(ids[:, None, :], 1)[:, 0]
-    edges = lax.optimization_barrier((diffusivity[0, :1], diffusivity[0, lat_dev - 1 :], wanted))
+    edge_low, edge_high, first_row, final_row = last_edges(diffusivity, adjoint_end)
+    edges = lax.optimization_barrier((first_row, final_row, wanted))
     wanted = edges[2]
-    low = lax.ppermute(edges[1].astype(jnp.bfloat16), "lat", upward)
-    high = lax.ppermute(edges[0].astype(jnp.bfloat16), "lat", downward)
+    low = lax.ppermute(edges[1], "lat", upward)
+    high = lax.ppermute(edges[0], "lat", downward)
     found = gather(wanted, trajectory, slots)
-    edge_low, edge_high = last_edges(diffusivity, adjoint_end)
     returned, last_low = exchange(found, 2, edge_high, 1)
     terms = block_terms(
         slot, returned.reshape(devices * PAD, -1), obs_jac, obs_value, obs_weight, obs_valid

time: 127 us -> 123 us (0.969); the launches traced: 125 us -> 122 us
  local copies, waits for them, and re-layouts: 2.6 us -> 1.33 us
    pallas_call x1, Pallas kernels: 48.3 us -> 47 us  [chain(): pl.pallas_call(functools.partial(chain_kernel, lax.axis_size('tm'), lax.a...]
  transfers between devices with their start and end apart: 2 -> 2, of which waited for: 0 -> 0; matrix products, arithmetic and copies ran while one was open for 0% -> 0% of each run, Pallas kernels for 44% -> 42%
where the time goes in v4:
time: 123 us; the launch traced here: 122 us
  Pallas kernels  114 us (93%)
  starting transfers between devices  6.73 us (5%)
  local copies, waits for them, and re-layouts  1.33 us (1%)
    pallas_call x1, Pallas kernels, chain(): pl.pallas_call(functools.partial(chain_kernel, lax.axis_size('tm'), lax.a...  47 us
    pallas_call x2, Pallas kernels, exchange(): pl.pallas_call(functools.partial(exchange_kernel, count, lat, shift), out...  25.8 us
    pallas_call x1, Pallas kernels, exchange(): pl.pallas_call(functools.partial(exchange_kernel, count, lat, 0), out_sha...  9.73 us
    pallas_call x1, Pallas kernels, scatter(): pl.pallas_call(functools.partial(scatter_kernel, slots), out_shape=jax.Sh...  8.9 us
    pallas_call x1, Pallas kernels, gather(): pl.pallas_call(functools.partial(gather_kernel, slots), out_shape=jax.Sha...  8.66 us
    pallas_call x1, Pallas kernels, block_terms(): pl.pallas_call(blocks_kernel, out_shape=jax.ShapeDtypeStruct(states.shape...  7.76 us
    pallas_call x1, Pallas kernels, last_edges(): pl.pallas_call(last_edges_kernel, out_shape=(edge, edge, single, single),...  3.82 us
    ppermute x1, starting transfers between devices, per_device(): high = lax.ppermute(edges[0], 'lat', downward)  3.4 us
  transfers between devices with their start and end apart: 2, of which 0 were waited for; matrix products, arithmetic and copies ran while one was open for 0% of the time, Pallas kernels for 42%

profile of v4, /device:TPU:8, one launch (start us, length us, event | category | flops | bytes accessed | tf_op | source)
XLA Modules:
  0.0 122.5 jit_solution(8593048024827132134)
XLA Ops:
  0.0 2.7 %route.1 = (s32[32,128]{1,0:T(8,128)}, s32[96]{0:T(128)}) custom-call(s32[96]{0:T(128)} %bitcast.10, s32[96]{0:T(128)} %tile_ref.1), custom_call_target="tpu_custom_call" | custom-call | tf_op jit(solution)/shard_map/route/pallas_call | solution.py:43
  2.7 9.7 %exchange1.1 = s32[32,1,128]{2,1,0:T(1,128)} custom-call(s32[32,1,128]{2,1,0:T(1,128)} %bitcast.9), custom_call_target="tpu_custom_call" | custom-call | tf_op jit(solution)/shard_map/exchange1/pallas_call | solution.py:189
  12.4 3.8 %last_edges.1 = (bf16[2,64,2048]{2,1,0:T(8,128)(2,1)}, bf16[2,64,2048]{2,1,0:T(8,128)(2,1)}, bf16[1,64,2048]{2,1,0:T(8,128)(2,1)}, bf16[1,64,2048]{2,1,0:T(8,128)(2,1)}) custom-call(f32[1,4,64,2048]{3,2,1,0:T(8,128)} %coeff_ref.3, bf16[4,64,2048]{2,1,0:T(8,128)(2,1)} %end_ref.3), custom_call_target="tpu_custom_call" | custom-call | tf_op jit(solution)/shard_map/last_edges/pallas_call | solution.py:167
  16.2 3.3 %collective-permute-start = (bf16[1,64,2048]{2,1,0:T(8,128)(2,1)}, bf16[1,64,2048]{2,1,0:T(8,128)(2,1)S(1)}, u32[]{:S(2)}, u32[]{:S(2)}) collective-permute-start(bf16[1,64,2048]{2,1,0:T(8,128)(2,1)} %get-tuple-element.21), channel_id=1, source_target_pairs={{0,1},{1,2},{2,3},{3,4},{4,5},{5,6},{6,7},{8,9},{9,10},{10,11},{11... | collective-permute-start | bytes 786440 | tf_op jit(solution)/shard_map/ppermute | solution.py:537
  19.6 3.4 %collective-permute-start.1 = (bf16[1,64,2048]{2,1,0:T(8,128)(2,1)}, bf16[1,64,2048]{2,1,0:T(8,128)(2,1)S(1)}, u32[]{:S(2)}, u32[]{:S(2)}) collective-permute-start(bf16[1,64,2048]{2,1,0:T(8,128)(2,1)} %get-tuple-element.22), channel_id=1, source_target_pairs={{1,0},{2,1},{3,2},{4,3},{5,4},{6,5},{7,6},{9,8},{10,9},{11,10},{12... | collective-permute-start | bytes 786440 | tf_op jit(solution)/shard_map/ppermute | solution.py:538
  23.0 8.7 %gather.1.refs_0_ = f32[32,8,128]{2,1,0:T(8,128)} custom-call(s32[32,128]{1,0:T(8,128)} %bitcast.6, f32[1,4,64,2048]{3,2,1,0:T(8,128)} %traj_ref.1), custom_call_target="tpu_custom_call" | custom-call | tf_op jit(solution)/shard_map/gather/pallas_call | solution.py:237
  31.6 11.0 %exchange2.1 = (f32[32,8,128]{2,1,0:T(8,128)}, bf16[2,64,2048]{2,1,0:T(8,128)(2,1)}) custom-call(f32[32,8,128]{2,1,0:T(8,128)} %gather.1.refs_0_, bf16[2,64,2048]{2,1,0:T(8,128)(2,1)} %get-tuple-element.24.refs_1_), custom_call_target="tpu_custom_call" | custom-call | tf_op jit(solution)/shard_map/exchange2/pallas_call | solution.py:180
  42.6 7.8 %blocks.1 = f32[256,128]{1,0:T(8,128)} custom-call(s32[96]{0:T(128)} %get-tuple-element.26.slot_ref, f32[256,128]{1,0:T(8,128)} %bitcast.8, bf16[96,128,128]{2,1,0:T(8,128)(2,1)} %jac_ref.1, f32[96,128]{1,0:T(8,128)} %value_ref.1, f32[96,128]{1,0:T(8,128)} %weight_ref.1, s32[96,128]{1,0:T(8,128)} %valid_ref.1), custom_call_target="tpu_custom_call" | custom-call | tf_op jit(solution)/shard_map/blocks/pallas_call | solution.py:282
  50.4 0.0 copy-start
  50.4 0.0 copy-start.1
  50.4 14.8 %exchange3.1 = (f32[32,8,128]{2,1,0:T(8,128)}, bf16[2,64,2048]{2,1,0:T(8,128)(2,1)}) custom-call(f32[32,8,128]{2,1,0:T(8,128)} %bitcast.5, bf16[2,64,2048]{2,1,0:T(8,128)(2,1)} %get-tuple-element.28.refs_1_), custom_call_target="tpu_custom_call" | custom-call | tf_op jit(solution)/shard_map/exchange3/pallas_call | solution.py:180
  65.3 0.0 copy-start.2
  65.3 8.9 %scatter.1.forcing_ref = f32[4,64,2048]{2,1,0:T(8,128)} custom-call(s32[32,128]{1,0:T(8,128)} %bitcast.7, f32[32,8,128]{2,1,0:T(8,128)} %get-tuple-element.30.terms_ref), custom_call_target="tpu_custom_call" | custom-call | tf_op jit(solution)/shard_map/scatter/pallas_call | solution.py:313
  74.2 0.0 collective-permute-done.low_ref
  74.2 0.0 collective-permute-done.1.high_ref
  74.2 0.0 copy-done
  74.2 0.0 copy-done.1
  74.2 0.0 copy-done.2
  74.2 47.0 %chain.1 = f32[1,4,64,2048]{3,2,1,0:T(8,128)S(1)} custom-call(f32[1,4,64,2048]{3,2,1,0:T(8,128)} %coeff_ref.3, bf16[1,64,2048]{2,1,0:T(8,128)(2,1)S(1)} %collective-permute-done.low_ref, bf16[1,64,2048]{2,1,0:T(8,128)(2,1)S(1)} %collective-permute-done.1.high_ref, bf16[2,64,2048]{2,1,0:T(8,128)(2,1)S(1)} %copy-done.1, bf16[2,64,2048]{2,1,0:T(8,128)(2,1)S(1)} %copy-done.2, ...), custom_call_target="tpu_custom_call" | custom-call | tf_op jit(solution)/shard_map/chain/pallas_call | solution.py:490
  121.2 1.3 %copy.11 = f32[1,4,64,2048]{3,2,1,0:T(8,128)} copy(f32[1,4,64,2048]{3,2,1,0:T(8,128)S(1)} %chain.1) | data formatting | bytes 4194304
Async XLA Ops:
  16.2 57.9 %collective-permute-start = (bf16[1,64,2048]{2,1,0:T(8,128)(2,1)}, bf16[1,64,2048]{2,1,0:T(8,128)(2,1)S(1)}, u32[]{:S(2)}, u32[]{:S(2)}) collective-permute-start(bf16[1,64,2048]{2,1,0:T(8,128)(2,1)} %get-tuple-element.21), channel_id=1, source_target_pairs={{0,1},{1,2},{2,3},{3,4},{4,5},{5,6},{6,7},{8,9},{9,10},{10,11},{11... | collective-permute-start | bytes 786440 | tf_op jit(solution)/shard_map/ppermute | solution.py:537
  19.6 54.6 %collective-permute-start.1 = (bf16[1,64,2048]{2,1,0:T(8,128)(2,1)}, bf16[1,64,2048]{2,1,0:T(8,128)(2,1)S(1)}, u32[]{:S(2)}, u32[]{:S(2)}) collective-permute-start(bf16[1,64,2048]{2,1,0:T(8,128)(2,1)} %get-tuple-element.22), channel_id=1, source_target_pairs={{1,0},{2,1},{3,2},{4,3},{5,4},{6,5},{7,6},{9,8},{10,9},{11,10},{12... | collective-permute-start | bytes 786440 | tf_op jit(solution)/shard_map/ppermute | solution.py:538
  50.4 23.8 %copy-start = (bf16[4,64,2048]{2,1,0:T(8,128)(2,1)S(1)}, bf16[4,64,2048]{2,1,0:T(8,128)(2,1)}, u32[]{:S(2)}) copy-start(bf16[4,64,2048]{2,1,0:T(8,128)(2,1)} %end_ref.3) | copy-start | bytes 3145732
  50.4 23.8 %copy-start.1 = (bf16[2,64,2048]{2,1,0:T(8,128)(2,1)S(1)}, bf16[2,64,2048]{2,1,0:T(8,128)(2,1)}, u32[]{:S(2)}) copy-start(bf16[2,64,2048]{2,1,0:T(8,128)(2,1)} %get-tuple-element.25.last_low_ref) | copy-start | bytes 1572868
  65.3 8.9 %copy-start.2 = (bf16[2,64,2048]{2,1,0:T(8,128)(2,1)S(1)}, bf16[2,64,2048]{2,1,0:T(8,128)(2,1)}, u32[]{:S(2)}) copy-start(bf16[2,64,2048]{2,1,0:T(8,128)(2,1)} %get-tuple-element.29.last_high_ref) | copy-start | bytes 1572868

commit v5 on v4

--- a/solution.py
+++ b/solution.py
@@ -11,7 +11,7 @@
 SUB = 2
 LANES = 128
 PAD = 8
-CHUNK = 8
+CHUNK = 16
 MESH = pl.DeviceIdType.MESH
 VMEM = pl.BlockSpec(memory_space=pltpu.VMEM)
 SMEM = pl.BlockSpec(memory_space=pltpu.SMEM)

time: 123 us -> 129 us (1.049)
  Pallas kernels: 114 us -> 119 us
    pallas_call x1, Pallas kernels: 47 us -> 51.7 us  [chain(): pl.pallas_call(functools.partial(chain_kernel, lax.axis_size('tm'), lax.a...]
  transfers between devices with their start and end apart: 2 -> 2, of which waited for: 0 -> 0; matrix products, arithmetic and copies ran while one was open for 0% -> 0% of each run, Pallas kernels for 42% -> 40%
where the time goes in v5:
time: 129 us; the launch traced here: 127 us
  Pallas kernels  119 us (92%)
  starting transfers between devices  6.73 us (5%)
  local copies, waits for them, and re-layouts  1.33 us (1%)
    pallas_call x1, Pallas kernels, chain(): pl.pallas_call(functools.partial(chain_kernel, lax.axis_size('tm'), lax.a...  51.7 us
    pallas_call x2, Pallas kernels, exchange(): pl.pallas_call(functools.partial(exchange_kernel, count, lat, shift), out...  25.8 us
    pallas_call x1, Pallas kernels, exchange(): pl.pallas_call(functools.partial(exchange_kernel, count, lat, 0), out_sha...  9.73 us
    pallas_call x1, Pallas kernels, scatter(): pl.pallas_call(functools.partial(scatter_kernel, slots), out_shape=jax.Sh...  8.9 us
    pallas_call x1, Pallas kernels, gather(): pl.pallas_call(functools.partial(gather_kernel, slots), out_shape=jax.Sha...  8.66 us
    pallas_call x1, Pallas kernels, block_terms(): pl.pallas_call(blocks_kernel, out_shape=jax.ShapeDtypeStruct(states.shape...  7.76 us
    pallas_call x1, Pallas kernels, last_edges(): pl.pallas_call(last_edges_kernel, out_shape=(edge, edge, single, single),...  3.82 us
    ppermute x1, starting transfers between devices, per_device(): high = lax.ppermute(edges[0], 'lat', downward)  3.4 us
  transfers between devices with their start and end apart: 2, of which 0 were waited for; matrix products, arithmetic and copies ran while one was open for 0% of the time, Pallas kernels for 40%

profile of v5, /device:TPU:8, one launch (start us, length us, event | category | flops | bytes accessed | tf_op | source)
XLA Modules:
  0.0 127.3 jit_solution(15558418736885609131)
XLA Ops:
  0.0 2.7 %route.1 = (s32[32,128]{1,0:T(8,128)}, s32[96]{0:T(128)}) custom-call(s32[96]{0:T(128)} %bitcast.10, s32[96]{0:T(128)} %tile_ref.1), custom_call_target="tpu_custom_call" | custom-call | tf_op jit(solution)/shard_map/route/pallas_call | solution.py:43
  2.7 9.7 %exchange1.1 = s32[32,1,128]{2,1,0:T(1,128)} custom-call(s32[32,1,128]{2,1,0:T(1,128)} %bitcast.9), custom_call_target="tpu_custom_call" | custom-call | tf_op jit(solution)/shard_map/exchange1/pallas_call | solution.py:189
  12.4 3.8 %last_edges.1 = (bf16[2,64,2048]{2,1,0:T(8,128)(2,1)}, bf16[2,64,2048]{2,1,0:T(8,128)(2,1)}, bf16[1,64,2048]{2,1,0:T(8,128)(2,1)}, bf16[1,64,2048]{2,1,0:T(8,128)(2,1)}) custom-call(f32[1,4,64,2048]{3,2,1,0:T(8,128)} %coeff_ref.3, bf16[4,64,2048]{2,1,0:T(8,128)(2,1)} %end_ref.3), custom_call_target="tpu_custom_call" | custom-call | tf_op jit(solution)/shard_map/last_edges/pallas_call | solution.py:167
  16.2 3.3 %collective-permute-start = (bf16[1,64,2048]{2,1,0:T(8,128)(2,1)}, bf16[1,64,2048]{2,1,0:T(8,128)(2,1)S(1)}, u32[]{:S(2)}, u32[]{:S(2)}) collective-permute-start(bf16[1,64,2048]{2,1,0:T(8,128)(2,1)} %get-tuple-element.21), channel_id=1, source_target_pairs={{0,1},{1,2},{2,3},{3,4},{4,5},{5,6},{6,7},{8,9},{9,10},{10,11},{11... | collective-permute-start | bytes 786440 | tf_op jit(solution)/shard_map/ppermute | solution.py:537
  19.6 3.4 %collective-permute-start.1 = (bf16[1,64,2048]{2,1,0:T(8,128)(2,1)}, bf16[1,64,2048]{2,1,0:T(8,128)(2,1)S(1)}, u32[]{:S(2)}, u32[]{:S(2)}) collective-permute-start(bf16[1,64,2048]{2,1,0:T(8,128)(2,1)} %get-tuple-element.22), channel_id=1, source_target_pairs={{1,0},{2,1},{3,2},{4,3},{5,4},{6,5},{7,6},{9,8},{10,9},{11,10},{12... | collective-permute-start | bytes 786440 | tf_op jit(solution)/shard_map/ppermute | solution.py:538
  23.0 8.7 %gather.1.refs_0_ = f32[32,8,128]{2,1,0:T(8,128)} custom-call(s32[32,128]{1,0:T(8,128)} %bitcast.6, f32[1,4,64,2048]{3,2,1,0:T(8,128)} %traj_ref.1), custom_call_target="tpu_custom_call" | custom-call | tf_op jit(solution)/shard_map/gather/pallas_call | solution.py:237
  31.6 11.0 %exchange2.1 = (f32[32,8,128]{2,1,0:T(8,128)}, bf16[2,64,2048]{2,1,0:T(8,128)(2,1)}) custom-call(f32[32,8,128]{2,1,0:T(8,128)} %gather.1.refs_0_, bf16[2,64,2048]{2,1,0:T(8,128)(2,1)} %get-tuple-element.24.refs_1_), custom_call_target="tpu_custom_call" | custom-call | tf_op jit(solution)/shard_map/exchange2/pallas_call | solution.py:180
  42.6 7.8 %blocks.1 = f32[256,128]{1,0:T(8,128)} custom-call(s32[96]{0:T(128)} %get-tuple-element.26.slot_ref, f32[256,128]{1,0:T(8,128)} %bitcast.8, bf16[96,128,128]{2,1,0:T(8,128)(2,1)} %jac_ref.1, f32[96,128]{1,0:T(8,128)} %value_ref.1, f32[96,128]{1,0:T(8,128)} %weight_ref.1, s32[96,128]{1,0:T(8,128)} %valid_ref.1), custom_call_target="tpu_custom_call" | custom-call | tf_op jit(solution)/shard_map/blocks/pallas_call | solution.py:282
  50.4 0.0 copy-start
  50.4 0.0 copy-start.1
  50.4 14.8 %exchange3.1 = (f32[32,8,128]{2,1,0:T(8,128)}, bf16[2,64,2048]{2,1,0:T(8,128)(2,1)}) custom-call(f32[32,8,128]{2,1,0:T(8,128)} %bitcast.5, bf16[2,64,2048]{2,1,0:T(8,128)(2,1)} %get-tuple-element.28.refs_1_), custom_call_target="tpu_custom_call" | custom-call | tf_op jit(solution)/shard_map/exchange3/pallas_call | solution.py:180
  65.2 0.0 copy-start.2
  65.3 8.9 %scatter.1.forcing_ref = f32[4,64,2048]{2,1,0:T(8,128)} custom-call(s32[32,128]{1,0:T(8,128)} %bitcast.7, f32[32,8,128]{2,1,0:T(8,128)} %get-tuple-element.30.terms_ref), custom_call_target="tpu_custom_call" | custom-call | tf_op jit(solution)/shard_map/scatter/pallas_call | solution.py:313
  74.2 0.0 collective-permute-done.low_ref
  74.2 0.0 collective-permute-done.1.high_ref
  74.2 0.0 copy-done
  74.2 0.0 copy-done.1
  74.2 0.0 copy-done.2
  74.2 51.7 %chain.1 = f32[1,4,64,2048]{3,2,1,0:T(8,128)S(1)} custom-call(f32[1,4,64,2048]{3,2,1,0:T(8,128)} %coeff_ref.3, bf16[1,64,2048]{2,1,0:T(8,128)(2,1)S(1)} %collective-permute-done.low_ref, bf16[1,64,2048]{2,1,0:T(8,128)(2,1)S(1)} %collective-permute-done.1.high_ref, bf16[2,64,2048]{2,1,0:T(8,128)(2,1)S(1)} %copy-done.1, bf16[2,64,2048]{2,1,0:T(8,128)(2,1)S(1)} %copy-done.2, ...), custom_call_target="tpu_custom_call" | custom-call | tf_op jit(solution)/shard_map/chain/pallas_call | solution.py:490
  125.9 1.3 %copy.11 = f32[1,4,64,2048]{3,2,1,0:T(8,128)} copy(f32[1,4,64,2048]{3,2,1,0:T(8,128)S(1)} %chain.1) | data formatting | bytes 4194304
Async XLA Ops:
  16.2 57.9 %collective-permute-start = (bf16[1,64,2048]{2,1,0:T(8,128)(2,1)}, bf16[1,64,2048]{2,1,0:T(8,128)(2,1)S(1)}, u32[]{:S(2)}, u32[]{:S(2)}) collective-permute-start(bf16[1,64,2048]{2,1,0:T(8,128)(2,1)} %get-tuple-element.21), channel_id=1, source_target_pairs={{0,1},{1,2},{2,3},{3,4},{4,5},{5,6},{6,7},{8,9},{9,10},{10,11},{11... | collective-permute-start | bytes 786440 | tf_op jit(solution)/shard_map/ppermute | solution.py:537
  19.6 54.6 %collective-permute-start.1 = (bf16[1,64,2048]{2,1,0:T(8,128)(2,1)}, bf16[1,64,2048]{2,1,0:T(8,128)(2,1)S(1)}, u32[]{:S(2)}, u32[]{:S(2)}) collective-permute-start(bf16[1,64,2048]{2,1,0:T(8,128)(2,1)} %get-tuple-element.22), channel_id=1, source_target_pairs={{1,0},{2,1},{3,2},{4,3},{5,4},{6,5},{7,6},{9,8},{10,9},{11,10},{12... | collective-permute-start | bytes 786440 | tf_op jit(solution)/shard_map/ppermute | solution.py:538
  50.4 23.8 %copy-start = (bf16[4,64,2048]{2,1,0:T(8,128)(2,1)S(1)}, bf16[4,64,2048]{2,1,0:T(8,128)(2,1)}, u32[]{:S(2)}) copy-start(bf16[4,64,2048]{2,1,0:T(8,128)(2,1)} %end_ref.3) | copy-start | bytes 3145732
  50.4 23.8 %copy-start.1 = (bf16[2,64,2048]{2,1,0:T(8,128)(2,1)S(1)}, bf16[2,64,2048]{2,1,0:T(8,128)(2,1)}, u32[]{:S(2)}) copy-start(bf16[2,64,2048]{2,1,0:T(8,128)(2,1)} %get-tuple-element.25.last_low_ref) | copy-start | bytes 1572868
  65.2 8.9 %copy-start.2 = (bf16[2,64,2048]{2,1,0:T(8,128)(2,1)S(1)}, bf16[2,64,2048]{2,1,0:T(8,128)(2,1)}, u32[]{:S(2)}) copy-start(bf16[2,64,2048]{2,1,0:T(8,128)(2,1)} %get-tuple-element.29.last_high_ref) | copy-start | bytes 1572868
